TPU v7x, 32 devices: a whole 2x2x4 slice. The times are simulated.
32 devices in a mesh: dp: 8 (over z, x), tensor: 4 (over y, core).
Axes of the slice: x: 2, y: 2, z: 4, core: 2. Of those that a mesh axis runs over, the one named last changes fastest.
Arguments:
- streams: bfloat16 [128, 4, 7168], P('dp', None, 'tensor'), may hold values from -12 to 12
- mix_weight: bfloat16 [24, 4, 7168], P(None, None, 'tensor'), may hold values from -0.0625 to 0.0625
- mix_bias: float32 [24], replicated, may hold values from -4 to 4
- gate_weight: bfloat16 [18432, 7168], P('dp', 'tensor'), may hold values from -0.0625 to 0.0625
- up_weight: bfloat16 [18432, 7168], P('dp', 'tensor'), may hold values from -0.0625 to 0.0625
- down_weight: bfloat16 [18432, 7168], P('dp', 'tensor'), may hold values from -0.046875 to 0.046875
Outputs:
- new_streams: bfloat16 [128, 4, 7168], P('dp', None, 'tensor')
All inputs are finite; a program needn't handle non-finite values.
Results may differ from a plain program's by a relative error of at most 0.006.
The roundings to bfloat16 on the way count: a program that leaves them out, or rounds other values in their place, can miss the bound.
Values may be sent and summed in bfloat16 or wider, within the bound.
No kernel may reach another device: no remote copies, remote signals or barrier semaphores. Data moves between devices by JAX's collectives and lax.ppermute only.
A program may use at most 64 MiB of HBM per device.

v0:
```python
import jax
import jax.numpy as jnp
from jax import lax
from jax.sharding import PartitionSpec as P

D = 7168
ITERS = 20


epsilon = 1e-06


def normalize(sweep_index, matrix):
    matrix = matrix / jnp.sum(matrix, axis=2, keepdims=True)
    return matrix / jnp.sum(matrix, axis=1, keepdims=True)


def mixing(raw_logits, squares, mix_bias, stream_count):
    scale_inv = lax.rsqrt(squares / (stream_count * D) + epsilon)
    logits = raw_logits * scale_inv[:, None] + mix_bias[None, :]
    pre_gate = jax.nn.sigmoid(logits[:, :stream_count])
    post_gate = 2.0 * jax.nn.sigmoid(logits[:, stream_count : 2 * stream_count])
    matrix = jnp.exp(logits[:, 2 * stream_count :]).reshape(-1, stream_count, stream_count)
    matrix = lax.fori_loop(0, ITERS, normalize, matrix)
    return (pre_gate, post_gate, matrix)


def contract_last(weights, rows):
    return lax.dot_general(
        weights, rows, (((1,), (1,)), ((), ())), preferred_element_type=jnp.float32
    )


def per_device(streams, mix_weight, mix_bias, gate_weight, up_weight, down_weight):
    tok_rows, stream_count, width_local = streams.shape
    logit_count = mix_weight.shape[0]
    flat_rows = streams.reshape(tok_rows, stream_count * width_local)
    flat_weight = mix_weight.reshape(logit_count, stream_count * width_local)
    raw_logits = lax.dot_general(
        flat_rows, flat_weight, (((1,), (1,)), ((), ())), preferred_element_type=jnp.float32
    )
    stream_wide = streams.astype(jnp.float32)
    squares = jnp.sum(stream_wide * stream_wide, axis=(1, 2))
    total_logits, total_squares = lax.psum((raw_logits, squares), "tensor")
    pre_gate, post_gate, res_mix = mixing(total_logits, total_squares, mix_bias, stream_count)
    mlp_input = jnp.einsum(
        "ts,tsc->tc", pre_gate, stream_wide, precision=lax.Precision.HIGHEST
    ).astype(jnp.bfloat16)
    unit_local = gate_weight.shape[0]
    block_rows = lax.all_gather(mlp_input, "dp", axis=0, tiled=True)
    gate_part = contract_last(gate_weight, block_rows)
    up_part = contract_last(up_weight, block_rows)
    both_parts = jnp.concatenate((gate_part, up_part), axis=0)
    unit_share = lax.psum_scatter(both_parts, "tensor", scatter_dimension=1, tiled=True)
    hidden_share = (jax.nn.silu(unit_share[:unit_local]) * unit_share[unit_local:]).astype(
        jnp.bfloat16
    )
    hidden = lax.all_gather(hidden_share, "tensor", axis=1, tiled=True)
    mlp_out = lax.psum_scatter(
        lax.dot_general(
            hidden, down_weight, (((0,), (0,)), ((), ())), preferred_element_type=jnp.float32
        ),
        "dp",
        scatter_dimension=0,
        tiled=True,
    )
    mixed = jnp.einsum("tij,tjc->tic", res_mix, stream_wide, precision=lax.Precision.HIGHEST)
    mixed = mixed + post_gate[:, :, None] * mlp_out[:, None, :]
    return mixed.astype(jnp.bfloat16)


def solution(mesh):
    in_specs = (
        P("dp", None, "tensor"),
        P(None, None, "tensor"),
        P(),
        P("dp", "tensor"),
        P("dp", "tensor"),
        P("dp", "tensor"),
    )
    out_specs = P("dp", None, "tensor")
    return jax.shard_map(
        per_device, mesh=mesh, in_specs=in_specs, out_specs=out_specs, check_vma=False
    )
```

profile of v0, /device:TPU:0, one launch (start us, length us, event | category | flops | bytes accessed | tf_op | source)
XLA Modules:
  0.0 182.8 jit_solution(2058229806804568332)
XLA Ops:
  6.5 0.0 copy-start
  6.5 0.0 reduce-scatter.3.cloned.1.call-start
  6.5 1.2 multiply_reduce_fusion
  7.8 0.0 copy-done
  7.8 1.2 convolution_bitcast_fusion.2
  8.9 8.7 %all-reduce = (f32[16,24]{1,0:T(8,128)S(1)}, f32[16]{0:T(128)S(1)}) all-reduce(f32[16,24]{1,0:T(8,128)S(1)} %convolution_bitcast_fusion.2, f32[16]{0:T(128)S(1)} %multiply_reduce_fusion), channel_id=1, replica_groups=mesh['dp'=8,'tensor'=4] {'tensor'}, use_global_device_ids=true, to_apply=%region_0.0 | all-reduce | flops 400 | bytes 3200 | tf_op jit(solution)/shard_map/psum | solution.py:44
  17.6 0.0 copy-start.1
  17.7 0.9 multiply_add_fusion
  18.5 0.1 fusion.10
  18.6 1.6 fusion.11
  20.3 31.8 %all_gather.6 = bf16[128,1792]{1,0:T(8,128)(2,1)S(1)} all-gather(bf16[16,1792]{1,0:T(8,128)(2,1)S(1)} %bitcast.24), channel_id=1, replica_groups=mesh['dp'=8,'tensor'=4] {'dp'}, dimensions={0}, use_global_device_ids=true | all-gather | bytes 516096 | tf_op jit(solution)/shard_map/all_gather | solution.py:50
  52.1 6.1 %convolution_bitcast_fusion = f32[2304,128]{0,1:T(8,128)S(1)} fusion(bf16[128,1792]{1,0:T(8,128)(2,1)S(1)} %all_gather.6, bf16[2304,1792]{1,0:T(8,128)(2,1)} %param.12), kind=kOutput, calls=%fused_computation.2 | convolution fusion | flops 1056964608 | bytes 9895936 | tf_op jit(solution)/shard_map/dot_general | solution.py:29
  58.2 0.0 copy-done.1
  58.2 2.8 %convolution_bitcast_fusion.1 = f32[2304,128]{0,1:T(8,128)S(1)} fusion(bf16[128,1792]{1,0:T(8,128)(2,1)S(1)} %all_gather.6, bf16[2304,1792]{1,0:T(8,128)(2,1)S(1)} %copy-done.1), kind=kOutput, calls=%fused_computation.3 | convolution fusion | flops 1056964608 | bytes 9895936 | tf_op jit(solution)/shard_map/dot_general | solution.py:29
  61.0 1.7 pad_maximum_fusion
  62.7 0.0 reduce-scatter.3.cloned.1.call-update
  62.7 0.0 reduce-scatter.5.cloned.1.call-start
  62.7 0.1 slice_exponential_fusion
  62.8 0.1 copy.13
  62.9 32.5 %reduce-scatter.3.cloned.1.call-done = f32[4608,32]{0,1:T(8,128)} async-done(((f32[4608,128]{0,1:T(8,128)}), f32[4608,32]{0,1:T(8,128)}) %reduce-scatter.3.cloned.1.call-update) | async-done | bytes 589840 | tf_op jit(solution)/shard_map/reduce_scatter | solution.py:54
  95.4 1.1 fusion.2
  96.6 7.0 %all_gather.7 = bf16[2304,128]{0,1:T(8,128)(2,1)S(1)} all-gather(bf16[2304,32]{0,1:T(8,128)(2,1)S(1)} %fusion.2), channel_id=1, replica_groups=mesh['dp'=8,'tensor'=4] {'tensor'}, dimensions={1}, use_global_device_ids=true | all-gather | bytes 737280 | tf_op jit(solution)/shard_map/all_gather | solution.py:58
  103.5 0.0 copy-start.2
  103.5 5.6 %fusion.12 = f32[128,1792]{1,0:T(8,128)} fusion(bf16[2304,128]{0,1:T(8,128)(2,1)S(1)} %all_gather.7, bf16[2304,1792]{1,0:T(8,128)(2,1)} %param.13), kind=kOutput, calls=%fused_computation.27 | convolution fusion | flops 1056964608 | bytes 9764864 | tf_op jit(solution)/shard_map/dot_general | solution.py:60
  109.1 0.0 reduce-scatter.5.cloned.1.call-update
  109.1 1.5 while.10
  110.7 0.1 copy.14
  110.8 63.1 %reduce-scatter.5.cloned.1.call-done = f32[16,1792]{1,0:T(8,128)} async-done(((f32[128,1792]{1,0:T(8,128)}), f32[16,1792]{1,0:T(8,128)}) %reduce-scatter.5.cloned.1.call-update) | async-done | bytes 114704 | tf_op jit(solution)/shard_map/reduce_scatter | solution.py:59
  173.8 0.0 copy-done.2
  173.9 2.1 %fusion = bf16[16,4,1792]{2,1,0:T(4,128)(2,1)} fusion(f32[16,4,4]{2,1,0:T(4,128)S(1)} %copy.14, bf16[16,4,1792]{2,1,0:T(4,128)(2,1)S(1)} %copy-done.2, f32[16,1792]{1,0:T(8,128)} %reduce-scatter.5.cloned.1.call-done, f32[16,4]{1,0:T(8,128)S(1)} %get-tuple-element.26), kind=kOutput, calls=%fused_computation.6 | convolution fusion | flops 5849088 | bytes 574720 | tf_op jit(solution)/shard_map/tij,tjc->tic/dot_general | solution.py:67
  (62 shorter events, 1.2 us)
Async XLA Ops:
  6.5 1.2 copy-start
  6.5 88.9 %reduce-scatter.3.cloned.1.call-start = ((), (), s32[]{:S(2)}) async-start(), calls=%async_computation.2 | async-start | bytes 2949120 | tf_op jit(solution)/shard_map/reduce_scatter | solution.py:54
  17.6 40.6 %copy-start.1 = (bf16[2304,1792]{1,0:T(8,128)(2,1)S(1)}, bf16[2304,1792]{1,0:T(8,128)(2,1)}, u32[]{:S(2)}) copy-start(bf16[2304,1792]{1,0:T(8,128)(2,1)} %param.11) | copy-start | bytes 24772612
  62.7 111.2 %reduce-scatter.5.cloned.1.call-start = ((), (), s32[]{:S(2)}) async-start(), calls=%async_computation.3 | async-start | bytes 1032192 | tf_op jit(solution)/shard_map/reduce_scatter | solution.py:59
  103.5 70.3 %copy-start.2 = (bf16[16,4,1792]{2,1,0:T(4,128)(2,1)S(1)}, bf16[16,4,1792]{2,1,0:T(4,128)(2,1)}, u32[]{:S(2)}) copy-start(bf16[16,4,1792]{2,1,0:T(4,128)(2,1)} %param.8) | copy-start | bytes 688132
Sparse Core Ops, SparseCore 0:
  62.8 32.5 reduce-scatter.2
  109.3 64.5 reduce-scatter.4
where the time goes:
time: 183 us
  waiting for transfers between devices  95.6 us (52%)
  blocking collectives  47.5 us (26%)
  matrix products  19.4 us (11%)
  between operations  13.5 us (7%)
  other arithmetic  6.14 us (3%)
    reduce_scatter x1, waiting for transfers between devices, per_device(): lax.psum_scatter(lax.dot_general(hidden, down_weight, (((0,), (0,)), ((),...  63.1 us
    reduce_scatter x1, waiting for transfers between devices, per_device(): lax.psum_scatter(both_parts, 'tensor', scatter_dimension=1, tiled=True)  32.5 us
    all_gather x1, blocking collectives, per_device(): block_rows = lax.all_gather(mlp_input, 'dp', axis=0, tiled=True)  31.8 us
    dot_general x2, matrix products, contract_last(): lax.dot_general(weights, rows, (((1,), (1,)), ((), ())), preferred_elemen...  8.91 us
    psum x1, blocking collectives, per_device(): total_logits, total_squares = lax.psum((raw_logits, squares), 'tensor')  8.71 us
    all_gather x1, blocking collectives, per_device(): hidden = lax.all_gather(hidden_share, 'tensor', axis=1, tiled=True)  6.96 us
    dot_general x1, matrix products, per_device(): lax.dot_general(hidden, down_weight, (((0,), (0,)), ((), ())), preferred_...  5.59 us
  transfers between devices with their start and end apart: 2, of which 2 were waited for; matrix products, arithmetic and copies ran while one was open for 1% of the time, Pallas kernels for 0%

commit v1 on v0

v1 whole, which is shorter than its diff:
```python
import functools

import jax
import jax.numpy as jnp
from jax import lax
from jax.experimental import pallas as pl
from jax.experimental.pallas import tpu as pltpu
from jax.sharding import PartitionSpec as P


D = 7168
ITERS = 20
EPSILON = 1e-06
LANES = 128
CHUNKS = 3


F32 = jnp.float32
BF16 = jnp.bfloat16
IN_VMEM = pl.BlockSpec(memory_space=pltpu.VMEM)
IN_HBM = pl.BlockSpec(memory_space=pltpu.HBM)
IN_ANY = pl.BlockSpec(memory_space=pl.ANY)
COPIES = 4


def call(body, outs, specs, aliases=None, limit=8 << 20, flops=0, scratch=()):
    return pl.pallas_call(
        body,
        out_shape=outs,
        in_specs=specs,
        out_specs=jax.tree.map(lambda _: IN_VMEM, outs),
        scratch_shapes=scratch,
        input_output_aliases=aliases or {},
        compiler_params=pltpu.CompilerParams(vmem_limit_bytes=limit),
        cost_estimate=pl.CostEstimate(flops=flops, bytes_accessed=0, transcendentals=0),
    )


def in_hbm(value):
    return pltpu.with_memory_space_constraint(value, pltpu.HBM)


def flip(value, axis, bits):
    size = lax.axis_size(axis)
    return lax.ppermute(value, axis, [(i, i ^ bits) for i in range(size)])


def gather_tokens(rows):
    size = lax.axis_size("dp")
    bit = size // 2
    while bit > 2:
        rows = jnp.concatenate((rows, flip(rows, "dp", bit)), axis=0)
        bit //= 2
    others = [flip(rows, "dp", k) for k in range(1, 2 * bit)]
    return jnp.concatenate([rows] + others, axis=0), rows


def scatter_tokens(kept, got):
    size = lax.axis_size("dp")
    for part in got:
        kept = kept + part.astype(F32)
    bit = 4
    while bit < size:
        half = kept.shape[0] // 2
        part = flip(kept[half:].astype(BF16), "dp", bit)
        kept = kept[:half] + part.astype(F32)
        bit *= 2
    return kept


def nt(rows, weights, precision=None):
    return lax.dot_general(
        rows, weights, (((1,), (1,)), ((), ())), preferred_element_type=F32, precision=precision
    )


def logits_body(streams_hbm, weight_hbm, bias_hbm, out_ref, streams_ref, bias_ref, wide_ref, weight_ref, sems):
    tokens, streams, width = wide_ref.shape
    logits = weight_ref.shape[0]
    pairs = ((streams_hbm, wide_ref), (weight_hbm, weight_ref), (bias_hbm, bias_ref))
    copies = [pltpu.make_async_copy(a, b, sems.at[k]) for k, (a, b) in enumerate(pairs)]
    for copy in copies:
        copy.start()
    copies[0].wait()
    squares = jnp.zeros((tokens, width), F32)
    for s in range(streams):
        rows = wide_ref[:, s, :]
        streams_ref[s] = rows
        wide = rows.astype(F32)
        squares = squares + wide * wide
    out_ref[:, logits : logits + 1] = jnp.sum(squares, axis=1, keepdims=True)
    copies[1].wait()
    total = jnp.zeros((tokens, logits), F32)
    for s in range(streams):
        total = total + nt(streams_ref[s], weight_ref[:, s, :])
    out_ref[:, :logits] = total
    copies[2].wait()


def mix_body(partial_ref, bias_ref, streams_ref, logits_ref, rows_ref):
    streams, tokens, width = streams_ref.shape
    count = bias_ref.shape[1]
    total = jnp.sum(partial_ref[...], axis=0)
    scale = lax.rsqrt(total[:, count : count + 1] / (streams * D) + EPSILON)
    logits = total[:, :count] * scale + bias_ref[...]
    logits_ref[:, :count] = logits
    pre = jax.nn.sigmoid(logits[:, :streams])
    rows = jnp.zeros((tokens, width), F32)
    for s in range(streams):
        rows = rows + pre[:, s : s + 1] * streams_ref[s].astype(F32)
    rows_ref[...] = rows.astype(BF16)


def sinkhorn_body(after_ref, logits_ref, out_ref, *, streams):
    logits = logits_ref[...]
    turned = logits.T
    first = 2 * streams
    rows = [jnp.exp(turned[first + i * streams : first + (i + 1) * streams]) for i in range(streams)]
    for _ in range(ITERS):
        rows = [row / jnp.sum(row, axis=0, keepdims=True) for row in rows]
        columns = functools.reduce(jnp.add, rows)
        rows = [row / columns for row in rows]
    post = 2.0 * jax.nn.sigmoid(turned[streams : 2 * streams])
    spare = jnp.zeros((LANES - streams - streams * streams, turned.shape[1]), F32)
    out_ref[...] = jnp.concatenate([post] + rows + [spare], axis=0).T


def load_body(after_ref, weight_ref, out_ref, sems):
    count = sems.shape[0]
    rows = weight_ref.shape[0] // count
    copies = []
    for k in range(count):
        at = pl.ds(k * rows, rows)
        copies.append(pltpu.make_async_copy(weight_ref.at[at], out_ref.at[at], sems.at[k]))
    for copy in copies:
        copy.start()
    for copy in copies:
        copy.wait()


def load(weight, after):
    copies = 1 if weight.shape[0] % (16 * COPIES) else COPIES
    return call(
        load_body,
        jax.ShapeDtypeStruct(weight.shape, weight.dtype),
        [IN_ANY, IN_HBM],
        flops=int(3e9),
        limit=1 << 20,
        scratch=[pltpu.SemaphoreType.DMA((copies,))],
    )(after, in_hbm(weight))


def expand_body(after_ref, x_ref, gate_ref, up_ref, send_ref, keep_ref, *, start):
    low = lax.axis_index("tensor") % 2
    size = send_ref.shape[2]
    half = gate_ref.shape[0] // 2
    x = x_ref[...]
    for own, out in ((1 - low, send_ref), (low, keep_ref)):
        at = pl.ds(pl.multiple_of(own * half + start, 8), size)
        out[0] = nt(x, gate_ref[at, :]).astype(out.dtype)
        out[1] = nt(x, up_ref[at, :]).astype(out.dtype)


def add_body(keep_ref, got_ref, *refs):
    before, (sum_far, sent_far, sum_near, sent_near) = refs[:-4], refs[-4:]
    tokens = sum_far.shape[1]
    done = sum_near.shape[2] - keep_ref.shape[2]
    total = keep_ref[...] + got_ref[...].astype(F32)
    far, near = total[:, tokens:], total[:, :tokens]
    sum_far[...] = far
    sent_far[...] = far.astype(BF16)
    if done:
        sum_near[:, :, :done] = before[0][...]
        sent_near[:, :, :done] = before[1][...]
    sum_near[:, :, done:] = near
    sent_near[:, :, done:] = near.astype(BF16)


def hidden_body(after_ref, *refs):
    out_ref = refs[-1]
    at = 0
    for sum_ref, got_ref in zip(refs[:-1:2], refs[1:-1:2]):
        size = sum_ref.shape[2]
        gate = sum_ref[0] + got_ref[0].astype(F32)
        up = sum_ref[1] + got_ref[1].astype(F32)
        out_ref[:, at : at + size] = (jax.nn.silu(gate) * up).astype(BF16)
        at += size


def reduce_body(after_ref, mine_ref, other_ref, down_ref, *outs):
    low = lax.axis_index("tensor") % 2
    half = down_ref.shape[0] // 2
    total = None
    for own, rows in ((low, mine_ref), (1 - low, other_ref)):
        at = pl.ds(pl.multiple_of(own * half, 8), half)
        part = jnp.dot(rows[...], down_ref[at, :], preferred_element_type=F32)
        total = part if total is None else total + part
    at = 0
    for out_ref in outs:
        size = out_ref.shape[0]
        out_ref[...] = total[at : at + size].astype(out_ref.dtype)
        at += size


def pieces_of(half):
    if half % (CHUNKS * LANES):
        return [(0, half)]
    size = half // CHUNKS
    return [(k * size, size) for k in range(CHUNKS)]


def layer(streams, mix_weight, mix_bias, gate_weight, up_weight, down_weight):
    tokens, stream_count, width = streams.shape
    count = mix_weight.shape[0]
    shape = jax.ShapeDtypeStruct
    partial, turned, bias = call(
        logits_body,
        (
            shape((tokens, LANES), F32),
            shape((stream_count, tokens, width), BF16),
            shape((1, count), F32),
        ),
        [IN_HBM] * 3,
        scratch=[
            pltpu.VMEM(streams.shape, BF16),
            pltpu.VMEM(mix_weight.shape, BF16),
            pltpu.SemaphoreType.DMA((3,)),
        ],
    )(in_hbm(streams), in_hbm(mix_weight), in_hbm(mix_bias[None, :]))
    gathered = lax.all_gather(partial, "tensor")
    logits, rows = call(
        mix_body,
        (shape((tokens, LANES), F32), shape((tokens, width), BF16)),
        [IN_VMEM] * 3,
    )(gathered, bias, turned)

    gate = load(gate_weight, rows)
    rows, near_rows = gather_tokens(rows)
    up = load(up_weight, near_rows)
    every = rows.shape[0]
    part = every // 2
    tensor_size = lax.axis_size("tensor")
    pieces = pieces_of(gate_weight.shape[0] // 2)

    def across(total, sent):
        bit = 2
        while 2 * bit < tensor_size:
            total = total + flip(sent, "tensor", bit).astype(F32)
            sent = total.astype(BF16)
            bit *= 2
        return total, flip(sent, "tensor", bit)

    far, before = [], ()
    afters = [rows]
    for at, (start, size) in enumerate(pieces):
        send, keep = call(
            functools.partial(expand_body, start=start),
            (shape((2, every, size), BF16), shape((2, every, size), F32)),
            [IN_ANY] + [IN_VMEM] * 3,
            flops=8 * every * size * width,
        )(afters[max(0, at - 1)], rows, gate, up)
        got = flip(send, "tensor", 1)
        far_sum, far_sent, *before = call(
            add_body,
            (
                shape((2, part, size), F32),
                shape((2, part, size), BF16),
                shape((2, part, start + size), F32),
                shape((2, part, start + size), BF16),
            ),
            [IN_VMEM] * (2 + len(before)),
        )(keep, got, *before)
        afters.append(far_sent)
        far.append(across(far_sum, far_sent))
    near = across(*before)
    down = load(down_weight, before[1])

    def outward(pairs, after, outs):
        mine = call(
            hidden_body,
            shape((part, gate_weight.shape[0] // 2), BF16),
            [IN_ANY] + [IN_VMEM] * (2 * len(pairs)),
        )(after, *[x for pair in pairs for x in pair])
        other = flip(mine, "tensor", 1)
        return call(
            reduce_body,
            outs,
            [IN_ANY] + [IN_VMEM] * 3,
            flops=4 * part * gate_weight.shape[0] * width,
        )(after, mine, other, down)

    step = every // 4
    sent = [shape((step, width), BF16)] * 2
    two, three = outward(far, before[1], sent)
    got = [flip(two, "dp", 2), flip(three, "dp", 3)]
    kept, one = outward([near], two, [shape((step, width), F32), sent[0]])
    got.append(flip(one, "dp", 1))
    mlp_out = scatter_tokens(kept, got)
    mixing = call(
        functools.partial(sinkhorn_body, streams=stream_count),
        shape((tokens, LANES), F32),
        [IN_ANY, IN_VMEM],
        flops=int(1e9),
    )(kept, logits)
    post_gate = mixing[:, :stream_count]
    entries = mixing[:, stream_count : stream_count + stream_count**2]
    res_mix = entries.reshape(tokens, stream_count, stream_count)
    mixed = jnp.einsum(
        "tij,tjc->tic", res_mix, streams.astype(F32), precision=lax.Precision.HIGHEST
    )
    mixed = mixed + post_gate[:, :, None] * mlp_out[:, None, :]
    return mixed.astype(BF16)


def solution(mesh):
    in_specs = (
        P("dp", None, "tensor"),
        P(None, None, "tensor"),
        P(),
        P("dp", "tensor"),
        P("dp", "tensor"),
        P("dp", "tensor"),
    )
    out_specs = P("dp", None, "tensor")
    return jax.shard_map(layer, mesh=mesh, in_specs=in_specs, out_specs=out_specs, check_vma=False)
```

time: 183 us -> 64.8 us (0.35)
  waiting for transfers between devices: 95.6 us -> 16.7 us
  blocking collectives: 47.5 us -> 6.23 us
  Pallas kernels: 0 us -> 22.1 us
  matrix products: 19.4 us -> 1.22 us
  starting transfers between devices: 0.04 us -> 17.9 us
  between operations: 13.5 us -> 0.22 us
  other arithmetic: 6.14 us -> 0.07 us
    reduce_scatter x2 -> x0, waiting for transfers between devices: 95.6 us -> none  [the longest x1 63.1 us: per_device(): lax.psum_scatter(lax.dot_general(hidden, down_weight, (((0,), (0,)), ((),...]
    all_gather x2 -> x1, blocking collectives: 38.7 us -> 6.23 us  [layer(): gathered = lax.all_gather(partial, 'tensor')]
    pallas_call x0 -> x16, Pallas kernels: none -> 22.1 us  [the longest x3 10.4 us: load(): call(load_body, jax.ShapeDtypeStruct(weight.shape, weight.dtype), [IN_ANY...]
    dot_general x6 -> x1, matrix products: 19.4 us -> 1.22 us  [layer(): jnp.einsum('tij,tjc->tic', res_mix, streams.astype(F32), precision=lax.Pr...]
    ppermute x0 -> x17, starting transfers between devices: none -> 17.9 us  [flip(): return lax.ppermute(value, axis, [(i, i ^ bits) for i in range(size)])]
    ppermute x0 -> x17, waiting for transfers between devices: none -> 16.7 us  [flip(): return lax.ppermute(value, axis, [(i, i ^ bits) for i in range(size)])]
    psum x1 -> x0, blocking collectives: 8.71 us -> none  [per_device(): total_logits, total_squares = lax.psum((raw_logits, squares), 'tensor')]
    reduce_sum x41 -> x0, other arithmetic: 2.03 us -> none  [the longest x1 1.22 us: per_device(): squares = jnp.sum(stream_wide * stream_wide, axis=(1, 2))]
  transfers between devices with their start and end apart: 2 -> 17, of which waited for: 2 -> 8; matrix products, arithmetic and copies ran while one was open for 1% -> 0% of each run, Pallas kernels for 0% -> 27%
where the time goes in v1:
time: 64.8 us; the launch traced here: 64.7 us
  Pallas kernels  22.1 us (34%)
  starting transfers between devices  17.9 us (28%)
  waiting for transfers between devices  16.7 us (26%)
  blocking collectives  6.23 us (10%)
  matrix products  1.22 us (2%)
    ppermute x17, starting transfers between devices, flip(): return lax.ppermute(value, axis, [(i, i ^ bits) for i in range(size)])  17.9 us
    ppermute x17, waiting for transfers between devices, flip(): return lax.ppermute(value, axis, [(i, i ^ bits) for i in range(size)])  16.7 us
    pallas_call x3, Pallas kernels, load(): call(load_body, jax.ShapeDtypeStruct(weight.shape, weight.dtype), [IN_ANY...  10.4 us
    all_gather x1, blocking collectives, layer(): gathered = lax.all_gather(partial, 'tensor')  6.23 us
    pallas_call x3, Pallas kernels, layer(): call(functools.partial(expand_body, start=start), (shape((2, every, size)...  4.88 us
    pallas_call x2, Pallas kernels, outward(): call(reduce_body, outs, [IN_ANY] + [IN_VMEM] * 3, flops=4 * part * gate_w...  3.12 us
    pallas_call x1, Pallas kernels, layer(): call(logits_body, (shape((tokens, LANES), F32), shape((stream_count, toke...  2.41 us
  transfers between devices with their start and end apart: 17, of which 8 were waited for; matrix products, arithmetic and copies ran while one was open for 0% of the time, Pallas kernels for 27%

profile of v1, /device:TPU:0, one launch (start us, length us, event | category | flops | bytes accessed | tf_op | source)
XLA Modules:
  0.0 64.7 jit_solution(10941345646683584317)
XLA Ops:
  0.0 2.4 %shard_map.64 = (f32[16,128]{1,0:T(8,128)S(1)}, bf16[4,16,1792]{2,1,0:T(8,128)(2,1)S(1)}, f32[1,24]{1,0:T(1,128)S(1)}) custom-call(bf16[16,4,1792]{2,1,0:T(4,128)(2,1)} %streams_hbm.1, bf16[24,4,1792]{2,1,0:T(4,128)(2,1)} %weight_hbm.1, f32[1,24]{1,0:T(1,128)} %bitcast.9), custom_call_target="tpu_custom_call" | custom-call | tf_op jit(solution)/shard_map/pallas_call | solution.py:216
  2.4 6.2 %all-gather = f32[64,128]{1,0:T(8,128)S(1)} all-gather(f32[16,128]{1,0:T(8,128)S(1)} %get-tuple-element.32), channel_id=2, replica_groups=mesh['dp'=8,'tensor'=4] {'tensor'}, dimensions={0}, use_global_device_ids=true | all-gather | bytes 40960 | tf_op jit(solution)/shard_map/all_gather | solution.py:230
  8.9 3.1 %collective-permute-start = (bf16[16,1792]{1,0:T(8,128)(2,1)S(1)}, bf16[16,1792]{1,0:T(8,128)(2,1)S(1)}, u32[]{:S(2)}, u32[]{:S(2)}) collective-permute-start(bf16[16,1792]{1,0:T(8,128)(2,1)S(1)} %get-tuple-element.35.after_ref), channel_id=1, source_target_pairs={{0,16},{4,20},{8,24},{12,28},{16,0},{20,4},{24,8},{28,12},{1,17},{... | collective-permute-start | bytes 172040 | tf_op jit(solution)/shard_map/ppermute | solution.py:45
  11.9 3.5 %shard_map.66.gate_ref = bf16[2304,1792]{1,0:T(8,128)(2,1)S(1)} custom-call(bf16[16,1792]{1,0:T(8,128)(2,1)S(1)} %get-tuple-element.35.after_ref, bf16[2304,1792]{1,0:T(8,128)(2,1)} %weight_ref.3), custom_call_target="tpu_custom_call" | custom-call | flops 3000000000 | tf_op jit(solution)/shard_map/pallas_call | solution.py:143
  15.6 2.4 %collective-permute-start.3 = (bf16[32,1792]{1,0:T(8,128)(2,1)S(1)}, bf16[32,1792]{1,0:T(8,128)(2,1)S(1)}, u32[]{:S(2)}, u32[]{:S(2)}) collective-permute-start(bf16[32,1792]{1,0:T(8,128)(2,1)S(1)} %get-tuple-element.59.after_ref), channel_id=1, source_target_pairs={{0,12},{4,8},{8,4},{12,0},{16,28},{20,24},{24,20},{28,16},{1,13},{... | collective-permute-start | bytes 344072 | tf_op jit(solution)/shard_map/ppermute | solution.py:45
  18.0 0.7 %collective-permute-start.2 = (bf16[32,1792]{1,0:T(8,128)(2,1)S(1)}, bf16[32,1792]{1,0:T(8,128)(2,1)S(1)}, u32[]{:S(2)}, u32[]{:S(2)}) collective-permute-start(bf16[32,1792]{1,0:T(8,128)(2,1)S(1)} %get-tuple-element.59.after_ref), channel_id=1, source_target_pairs={{0,8},{4,12},{8,0},{12,4},{16,24},{20,28},{24,16},{28,20},{1,9},{5... | collective-permute-start | bytes 344072 | tf_op jit(solution)/shard_map/ppermute | solution.py:45
  18.7 0.5 collective-permute-start.1
  19.2 3.5 %shard_map.67.up_ref = bf16[2304,1792]{1,0:T(8,128)(2,1)S(1)} custom-call(bf16[32,1792]{1,0:T(8,128)(2,1)S(1)} %get-tuple-element.59.after_ref, bf16[2304,1792]{1,0:T(8,128)(2,1)} %weight_ref.4), custom_call_target="tpu_custom_call" | custom-call | flops 3000000000 | tf_op jit(solution)/shard_map/pallas_call | solution.py:143
  22.6 1.4 %collective-permute-done.1 = bf16[32,1792]{1,0:T(8,128)(2,1)S(1)} collective-permute-done((bf16[32,1792]{1,0:T(8,128)(2,1)S(1)}, bf16[32,1792]{1,0:T(8,128)(2,1)S(1)}, u32[]{:S(2)}, u32[]{:S(2)}) %collective-permute-start.1) | collective-permute-done | bytes 114720 | tf_op jit(solution)/shard_map/ppermute | solution.py:45
  24.1 1.6 %shard_map.68 = (bf16[2,128,384]{2,1,0:T(8,128)(2,1)S(1)}, f32[2,128,384]{2,1,0:T(8,128)S(1)}) custom-call(bf16[128,1792]{1,0:T(8,128)(2,1)S(1)} %constant_dynamic-update-slice_fusion.2.after_ref.x_ref, bf16[128,1792]{1,0:T(8,128)(2,1)S(1)} %constant_dynamic-update-slice_fusion.2.after_ref.x_ref, bf16[2304,1792]{1,0:T(8,128)(2,1)S(1)} %shard_map.66.gate_ref, ...), custom_call_target="tpu_custom_call" | custom-call | flops 704643072 | tf_op jit(solution)/shard_map/pallas_call | solution.py:256
  25.8 1.6 %shard_map.71 = (bf16[2,128,384]{2,1,0:T(8,128)(2,1)S(1)}, f32[2,128,384]{2,1,0:T(8,128)S(1)}) custom-call(bf16[128,1792]{1,0:T(8,128)(2,1)S(1)} %constant_dynamic-update-slice_fusion.2.after_ref.x_ref, bf16[128,1792]{1,0:T(8,128)(2,1)S(1)} %constant_dynamic-update-slice_fusion.2.after_ref.x_ref, bf16[2304,1792]{1,0:T(8,128)(2,1)S(1)} %shard_map.66.gate_ref, ...), custom_call_target="tpu_custom_call" | custom-call | flops 704643072 | tf_op jit(solution)/shard_map/pallas_call | solution.py:256
  27.4 0.5 collective-permute-start.6
  28.1 1.6 %shard_map.70 = (bf16[2,128,384]{2,1,0:T(8,128)(2,1)S(1)}, f32[2,128,384]{2,1,0:T(8,128)S(1)}) custom-call(bf16[2,64,384]{2,1,0:T(8,128)(2,1)S(1)} %get-tuple-element.38.after_ref, bf16[128,1792]{1,0:T(8,128)(2,1)S(1)} %constant_dynamic-update-slice_fusion.2.after_ref.x_ref, bf16[2304,1792]{1,0:T(8,128)(2,1)S(1)} %shard_map.66.gate_ref, ...), custom_call_target="tpu_custom_call" | custom-call | flops 704643072 | tf_op jit(solution)/shard_map/pallas_call | solution.py:256
  29.8 1.6 %collective-permute-start.7 = (bf16[2,64,384]{2,1,0:T(8,128)(2,1)S(1)}, bf16[2,64,384]{2,1,0:T(8,128)(2,1)S(1)}, u32[]{:S(2)}, u32[]{:S(2)}) collective-permute-start(bf16[2,64,384]{2,1,0:T(8,128)(2,1)S(1)} %get-tuple-element.38.after_ref), channel_id=1, source_target_pairs={{0,2},{1,3},{2,0},{3,1},{4,6},{5,7},{6,4},{7,5},{8,10},{9,11},{10,... | collective-permute-start | bytes 294920 | tf_op jit(solution)/shard_map/ppermute | solution.py:45
  31.5 0.5 collective-permute-start.8
  32.1 1.6 %collective-permute-start.9 = (bf16[2,64,384]{2,1,0:T(8,128)(2,1)S(1)}, bf16[2,64,384]{2,1,0:T(8,128)(2,1)S(1)}, u32[]{:S(2)}, u32[]{:S(2)}) collective-permute-start(bf16[2,64,384]{2,1,0:T(8,128)(2,1)S(1)} %get-tuple-element.52), channel_id=1, source_target_pairs={{0,2},{1,3},{2,0},{3,1},{4,6},{5,7},{6,4},{7,5},{8,10},{9,11},{10,... | collective-permute-start | bytes 294920 | tf_op jit(solution)/shard_map/ppermute | solution.py:45
  33.7 0.5 collective-permute-start.11
  34.2 3.4 %collective-permute-done.8.refs_3_ = bf16[2,64,384]{2,1,0:T(8,128)(2,1)S(1)} collective-permute-done((bf16[2,64,384]{2,1,0:T(8,128)(2,1)S(1)}, bf16[2,64,384]{2,1,0:T(8,128)(2,1)S(1)}, u32[]{:S(2)}, u32[]{:S(2)}) %collective-permute-start.8) | collective-permute-done | bytes 98336 | tf_op jit(solution)/shard_map/ppermute | solution.py:45
  37.6 2.1 %collective-permute-done.9.refs_5_ = bf16[2,64,384]{2,1,0:T(8,128)(2,1)S(1)} collective-permute-done((bf16[2,64,384]{2,1,0:T(8,128)(2,1)S(1)}, bf16[2,64,384]{2,1,0:T(8,128)(2,1)S(1)}, u32[]{:S(2)}, u32[]{:S(2)}) %collective-permute-start.9) | collective-permute-done | bytes 98336 | tf_op jit(solution)/shard_map/ppermute | solution.py:45
  39.9 3.5 %shard_map.75.down_ref = bf16[2304,1792]{1,0:T(8,128)(2,1)S(1)} custom-call(bf16[2,64,1152]{2,1,0:T(8,128)(2,1)S(1)} %get-tuple-element.47.after_ref, bf16[2304,1792]{1,0:T(8,128)(2,1)} %weight_ref.5), custom_call_target="tpu_custom_call" | custom-call | flops 3000000000 | tf_op jit(solution)/shard_map/pallas_call | solution.py:143
  43.4 1.6 %shard_map.76 = (bf16[32,1792]{1,0:T(8,128)(2,1)S(1)}, bf16[32,1792]{1,0:T(8,128)(2,1)S(1)}) custom-call(bf16[2,64,1152]{2,1,0:T(8,128)(2,1)S(1)} %get-tuple-element.47.after_ref, bf16[64,1152]{1,0:T(8,128)(2,1)S(1)} %shard_map.74.mine_ref, bf16[64,1152]{1,0:T(8,128)(2,1)S(1)} %collective-permute-done.10.other_ref, bf16[2304,1792]{1,0:T(8,128)(2,1)S(1)} %shard_map.75.down_ref), custom_call_target="tpu_custom_call" | custom-call | flops 1056964608 | tf_op jit(solution)/shard_map/pallas_call | solution.py:285
  45.0 0.5 collective-permute-done.11.refs_1_
  45.7 1.6 %collective-permute-start.13 = (bf16[32,1792]{1,0:T(8,128)(2,1)S(1)}, bf16[32,1792]{1,0:T(8,128)(2,1)S(1)}, u32[]{:S(2)}, u32[]{:S(2)}) collective-permute-start(bf16[32,1792]{1,0:T(8,128)(2,1)S(1)} %get-tuple-element.53.after_ref), channel_id=1, source_target_pairs={{0,8},{4,12},{8,0},{12,4},{16,24},{20,28},{24,16},{28,20},{1,9},{5... | collective-permute-start | bytes 344072 | tf_op jit(solution)/shard_map/ppermute | solution.py:45
  47.3 1.4 %collective-permute-start.14 = (bf16[32,1792]{1,0:T(8,128)(2,1)S(1)}, bf16[32,1792]{1,0:T(8,128)(2,1)S(1)}, u32[]{:S(2)}, u32[]{:S(2)}) collective-permute-start(bf16[32,1792]{1,0:T(8,128)(2,1)S(1)} %get-tuple-element.57), channel_id=1, source_target_pairs={{0,12},{4,8},{8,4},{12,0},{16,28},{20,24},{24,20},{28,16},{1,13},{... | collective-permute-start | bytes 344072 | tf_op jit(solution)/shard_map/ppermute | solution.py:45
  48.6 1.6 %shard_map.78 = (f32[32,1792]{1,0:T(8,128)S(1)}, bf16[32,1792]{1,0:T(8,128)(2,1)S(1)}) custom-call(bf16[32,1792]{1,0:T(8,128)(2,1)S(1)} %get-tuple-element.53.after_ref, bf16[64,1152]{1,0:T(8,128)(2,1)S(1)} %shard_map.77.mine_ref, bf16[64,1152]{1,0:T(8,128)(2,1)S(1)} %collective-permute-done.12.other_ref, bf16[2304,1792]{1,0:T(8,128)(2,1)S(1)} %shard_map.75.down_ref), custom_call_target="tpu_custom_call" | custom-call | flops 1056964608 | tf_op jit(solution)/shard_map/pallas_call | solution.py:285
  50.2 0.6 collective-permute-start.15
  50.9 3.8 %collective-permute-done.14 = bf16[32,1792]{1,0:T(8,128)(2,1)S(1)} collective-permute-done((bf16[32,1792]{1,0:T(8,128)(2,1)S(1)}, bf16[32,1792]{1,0:T(8,128)(2,1)S(1)}, u32[]{:S(2)}, u32[]{:S(2)}) %collective-permute-start.14) | collective-permute-done | bytes 114720 | tf_op jit(solution)/shard_map/ppermute | solution.py:45
  54.7 2.4 %collective-permute-done.15 = bf16[32,1792]{1,0:T(8,128)(2,1)S(1)} collective-permute-done((bf16[32,1792]{1,0:T(8,128)(2,1)S(1)}, bf16[32,1792]{1,0:T(8,128)(2,1)S(1)}, u32[]{:S(2)}, u32[]{:S(2)}) %collective-permute-start.15) | collective-permute-done | bytes 114720 | tf_op jit(solution)/shard_map/ppermute | solution.py:45
  57.1 2.6 %collective-permute-start.16 = (bf16[16,1792]{1,0:T(8,128)(2,1)S(1)}, bf16[16,1792]{1,0:T(8,128)(2,1)S(1)}, u32[]{:S(2)}, u32[]{:S(2)}) collective-permute-start(bf16[16,1792]{1,0:T(8,128)(2,1)S(1)} %slice.23), channel_id=1, source_target_pairs={{0,16},{4,20},{8,24},{12,28},{16,0},{20,4},{24,8},{28,12},{1,17},{... | collective-permute-start | bytes 172040 | tf_op jit(solution)/shard_map/ppermute | solution.py:45
  59.7 0.7 %shard_map.79 = f32[16,128]{1,0:T(8,128)S(1)} custom-call(f32[32,1792]{1,0:T(8,128)S(1)} %get-tuple-element.55.after_ref, f32[16,128]{1,0:T(8,128)S(1)} %get-tuple-element.56.logits_ref), custom_call_target="tpu_custom_call" | custom-call | flops 1000000000 | tf_op jit(solution)/shard_map/pallas_call | solution.py:299
  60.6 2.9 %collective-permute-done.16 = bf16[16,1792]{1,0:T(8,128)(2,1)S(1)} collective-permute-done((bf16[16,1792]{1,0:T(8,128)(2,1)S(1)}, bf16[16,1792]{1,0:T(8,128)(2,1)S(1)}, u32[]{:S(2)}, u32[]{:S(2)}) %collective-permute-start.16) | collective-permute-done | bytes 57376 | tf_op jit(solution)/shard_map/ppermute | solution.py:45
  63.5 1.2 %add_convert_fusion = bf16[16,4,1792]{2,1,0:T(4,128)(2,1)} fusion(f32[16,1792]{1,0:T(8,128)S(1)} %slice_add_fusion, f32[16,4]{1,0:T(8,128)S(1)} %bitcast.7, f32[16,4,4]{2,1,0:T(4,128)S(1)} %copy.8, bf16[16,4,1792]{2,1,0:T(4,128)(2,1)S(1)} %copy-done), kind=kOutput, calls=%fused_computation | convolution fusion | flops 5849088 | bytes 574720 | tf_op jit(solution)/shard_map/tij,tjc->tic/dot_general | solution.py:308
  (33 shorter events, 1.5 us)
Async XLA Ops:
  8.9 6.7 %collective-permute-start = (bf16[16,1792]{1,0:T(8,128)(2,1)S(1)}, bf16[16,1792]{1,0:T(8,128)(2,1)S(1)}, u32[]{:S(2)}, u32[]{:S(2)}) collective-permute-start(bf16[16,1792]{1,0:T(8,128)(2,1)S(1)} %get-tuple-element.35.after_ref), channel_id=1, source_target_pairs={{0,16},{4,20},{8,24},{12,28},{16,0},{20,4},{24,8},{28,12},{1,17},{... | collective-permute-start | bytes 172040 | tf_op jit(solution)/shard_map/ppermute | solution.py:45
  15.6 8.5 %collective-permute-start.3 = (bf16[32,1792]{1,0:T(8,128)(2,1)S(1)}, bf16[32,1792]{1,0:T(8,128)(2,1)S(1)}, u32[]{:S(2)}, u32[]{:S(2)}) collective-permute-start(bf16[32,1792]{1,0:T(8,128)(2,1)S(1)} %get-tuple-element.59.after_ref), channel_id=1, source_target_pairs={{0,12},{4,8},{8,4},{12,0},{16,28},{20,24},{24,20},{28,16},{1,13},{... | collective-permute-start | bytes 344072 | tf_op jit(solution)/shard_map/ppermute | solution.py:45
  18.0 6.0 %collective-permute-start.2 = (bf16[32,1792]{1,0:T(8,128)(2,1)S(1)}, bf16[32,1792]{1,0:T(8,128)(2,1)S(1)}, u32[]{:S(2)}, u32[]{:S(2)}) collective-permute-start(bf16[32,1792]{1,0:T(8,128)(2,1)S(1)} %get-tuple-element.59.after_ref), channel_id=1, source_target_pairs={{0,8},{4,12},{8,0},{12,4},{16,24},{20,28},{24,16},{28,20},{1,9},{5... | collective-permute-start | bytes 344072 | tf_op jit(solution)/shard_map/ppermute | solution.py:45
  18.7 5.3 %collective-permute-start.1 = (bf16[32,1792]{1,0:T(8,128)(2,1)S(1)}, bf16[32,1792]{1,0:T(8,128)(2,1)S(1)}, u32[]{:S(2)}, u32[]{:S(2)}) collective-permute-start(bf16[32,1792]{1,0:T(8,128)(2,1)S(1)} %get-tuple-element.59.after_ref), channel_id=1, source_target_pairs={{0,4},{4,0},{8,12},{12,8},{16,20},{20,16},{24,28},{28,24},{1,5},{5... | collective-permute-start | bytes 344072 | tf_op jit(solution)/shard_map/ppermute | solution.py:45
  25.7 2.3 %collective-permute-start.4 = (bf16[2,128,384]{2,1,0:T(8,128)(2,1)S(1)}, bf16[2,128,384]{2,1,0:T(8,128)(2,1)S(1)}, u32[]{:S(2)}, u32[]{:S(2)}) collective-permute-start(bf16[2,128,384]{2,1,0:T(8,128)(2,1)S(1)} %get-tuple-element.37), channel_id=1, source_target_pairs={{0,1},{1,0},{2,3},{3,2},{4,5},{5,4},{6,7},{7,6},{8,9},{9,8},{10,11... | collective-permute-start | bytes 589832 | tf_op jit(solution)/shard_map/ppermute | solution.py:45
  27.4 3.9 %collective-permute-start.6 = (bf16[2,128,384]{2,1,0:T(8,128)(2,1)S(1)}, bf16[2,128,384]{2,1,0:T(8,128)(2,1)S(1)}, u32[]{:S(2)}, u32[]{:S(2)}) collective-permute-start(bf16[2,128,384]{2,1,0:T(8,128)(2,1)S(1)} %get-tuple-element.42), channel_id=1, source_target_pairs={{0,1},{1,0},{2,3},{3,2},{4,5},{5,4},{6,7},{7,6},{8,9},{9,8},{10,11... | collective-permute-start | bytes 589832 | tf_op jit(solution)/shard_map/ppermute | solution.py:45
  29.7 2.3 %collective-permute-start.5 = (bf16[2,128,384]{2,1,0:T(8,128)(2,1)S(1)}, bf16[2,128,384]{2,1,0:T(8,128)(2,1)S(1)}, u32[]{:S(2)}, u32[]{:S(2)}) collective-permute-start(bf16[2,128,384]{2,1,0:T(8,128)(2,1)S(1)} %get-tuple-element.40), channel_id=1, source_target_pairs={{0,1},{1,0},{2,3},{3,2},{4,5},{5,4},{6,7},{7,6},{8,9},{9,8},{10,11... | collective-permute-start | bytes 589832 | tf_op jit(solution)/shard_map/ppermute | solution.py:45
  29.8 7.8 %collective-permute-start.7 = (bf16[2,64,384]{2,1,0:T(8,128)(2,1)S(1)}, bf16[2,64,384]{2,1,0:T(8,128)(2,1)S(1)}, u32[]{:S(2)}, u32[]{:S(2)}) collective-permute-start(bf16[2,64,384]{2,1,0:T(8,128)(2,1)S(1)} %get-tuple-element.38.after_ref), channel_id=1, source_target_pairs={{0,2},{1,3},{2,0},{3,1},{4,6},{5,7},{6,4},{7,5},{8,10},{9,11},{10,... | collective-permute-start | bytes 294920 | tf_op jit(solution)/shard_map/ppermute | solution.py:45
  31.5 6.1 %collective-permute-start.8 = (bf16[2,64,384]{2,1,0:T(8,128)(2,1)S(1)}, bf16[2,64,384]{2,1,0:T(8,128)(2,1)S(1)}, u32[]{:S(2)}, u32[]{:S(2)}) collective-permute-start(bf16[2,64,384]{2,1,0:T(8,128)(2,1)S(1)} %get-tuple-element.50), channel_id=1, source_target_pairs={{0,2},{1,3},{2,0},{3,1},{4,6},{5,7},{6,4},{7,5},{8,10},{9,11},{10,... | collective-permute-start | bytes 294920 | tf_op jit(solution)/shard_map/ppermute | solution.py:45
  32.1 7.6 %collective-permute-start.9 = (bf16[2,64,384]{2,1,0:T(8,128)(2,1)S(1)}, bf16[2,64,384]{2,1,0:T(8,128)(2,1)S(1)}, u32[]{:S(2)}, u32[]{:S(2)}) collective-permute-start(bf16[2,64,384]{2,1,0:T(8,128)(2,1)S(1)} %get-tuple-element.52), channel_id=1, source_target_pairs={{0,2},{1,3},{2,0},{3,1},{4,6},{5,7},{6,4},{7,5},{8,10},{9,11},{10,... | collective-permute-start | bytes 294920 | tf_op jit(solution)/shard_map/ppermute | solution.py:45
  33.7 11.8 %collective-permute-start.11 = (bf16[2,64,1152]{2,1,0:T(8,128)(2,1)S(1)}, bf16[2,64,1152]{2,1,0:T(8,128)(2,1)S(1)}, u32[]{:S(2)}, u32[]{:S(2)}) collective-permute-start(bf16[2,64,1152]{2,1,0:T(8,128)(2,1)S(1)} %get-tuple-element.47.after_ref), channel_id=1, source_target_pairs={{0,2},{1,3},{2,0},{3,1},{4,6},{5,7},{6,4},{7,5},{8,10},{9,11},{10,... | collective-permute-start | bytes 884744 | tf_op jit(solution)/shard_map/ppermute | solution.py:45
  39.8 3.6 %collective-permute-start.10 = (bf16[64,1152]{1,0:T(8,128)(2,1)S(1)}, bf16[64,1152]{1,0:T(8,128)(2,1)S(1)}, u32[]{:S(2)}, u32[]{:S(2)}) collective-permute-start(bf16[64,1152]{1,0:T(8,128)(2,1)S(1)} %shard_map.74.mine_ref), channel_id=1, source_target_pairs={{0,1},{1,0},{2,3},{3,2},{4,5},{5,4},{6,7},{7,6},{8,9},{9,8},{10,11... | collective-permute-start | bytes 442376 | tf_op jit(solution)/shard_map/ppermute | solution.py:45
  45.0 18.5 %copy-start = (bf16[16,4,1792]{2,1,0:T(4,128)(2,1)S(1)}, bf16[16,4,1792]{2,1,0:T(4,128)(2,1)}, u32[]{:S(2)}) copy-start(bf16[16,4,1792]{2,1,0:T(4,128)(2,1)} %streams_hbm.1) | copy-start | bytes 688132
  45.6 3.1 %collective-permute-start.12 = (bf16[64,1152]{1,0:T(8,128)(2,1)S(1)}, bf16[64,1152]{1,0:T(8,128)(2,1)S(1)}, u32[]{:S(2)}, u32[]{:S(2)}) collective-permute-start(bf16[64,1152]{1,0:T(8,128)(2,1)S(1)} %shard_map.77.mine_ref), channel_id=1, source_target_pairs={{0,1},{1,0},{2,3},{3,2},{4,5},{5,4},{6,7},{7,6},{8,9},{9,8},{10,11... | collective-permute-start | bytes 442376 | tf_op jit(solution)/shard_map/ppermute | solution.py:45
  45.7 9.0 %collective-permute-start.13 = (bf16[32,1792]{1,0:T(8,128)(2,1)S(1)}, bf16[32,1792]{1,0:T(8,128)(2,1)S(1)}, u32[]{:S(2)}, u32[]{:S(2)}) collective-permute-start(bf16[32,1792]{1,0:T(8,128)(2,1)S(1)} %get-tuple-element.53.after_ref), channel_id=1, source_target_pairs={{0,8},{4,12},{8,0},{12,4},{16,24},{20,28},{24,16},{28,20},{1,9},{5... | collective-permute-start | bytes 344072 | tf_op jit(solution)/shard_map/ppermute | solution.py:45
  47.3 7.4 %collective-permute-start.14 = (bf16[32,1792]{1,0:T(8,128)(2,1)S(1)}, bf16[32,1792]{1,0:T(8,128)(2,1)S(1)}, u32[]{:S(2)}, u32[]{:S(2)}) collective-permute-start(bf16[32,1792]{1,0:T(8,128)(2,1)S(1)} %get-tuple-element.57), channel_id=1, source_target_pairs={{0,12},{4,8},{8,4},{12,0},{16,28},{20,24},{24,20},{28,16},{1,13},{... | collective-permute-start | bytes 344072 | tf_op jit(solution)/shard_map/ppermute | solution.py:45
  50.2 6.8 %collective-permute-start.15 = (bf16[32,1792]{1,0:T(8,128)(2,1)S(1)}, bf16[32,1792]{1,0:T(8,128)(2,1)S(1)}, u32[]{:S(2)}, u32[]{:S(2)}) collective-permute-start(bf16[32,1792]{1,0:T(8,128)(2,1)S(1)} %get-tuple-element.58), channel_id=1, source_target_pairs={{0,4},{4,0},{8,12},{12,8},{16,20},{20,16},{24,28},{28,24},{1,5},{5... | collective-permute-start | bytes 344072 | tf_op jit(solution)/shard_map/ppermute | solution.py:45
  57.1 6.4 %collective-permute-start.16 = (bf16[16,1792]{1,0:T(8,128)(2,1)S(1)}, bf16[16,1792]{1,0:T(8,128)(2,1)S(1)}, u32[]{:S(2)}, u32[]{:S(2)}) collective-permute-start(bf16[16,1792]{1,0:T(8,128)(2,1)S(1)} %slice.23), channel_id=1, source_target_pairs={{0,16},{4,20},{8,24},{12,28},{16,0},{20,4},{24,8},{28,12},{1,17},{... | collective-permute-start | bytes 172040 | tf_op jit(solution)/shard_map/ppermute | solution.py:45

commit v2 on v1

--- a/solution.py
+++ b/solution.py
@@ -74,6 +74,13 @@
     )
 
 
+def group(count, streams):
+    shape = (count, count * streams)
+    row = lax.broadcasted_iota(jnp.int32, shape, 0)
+    column = lax.broadcasted_iota(jnp.int32, shape, 1)
+    return (column // streams == row).astype(F32)
+
+
 def logits_body(streams_hbm, weight_hbm, bias_hbm, out_ref, streams_ref, bias_ref, wide_ref, weight_ref, sems):
     tokens, streams, width = wide_ref.shape
     logits = weight_ref.shape[0]
@@ -82,25 +89,34 @@
     for copy in copies:
         copy.start()
     copies[0].wait()
-    squares = jnp.zeros((tokens, width), F32)
     for s in range(streams):
-        rows = wide_ref[:, s, :]
-        streams_ref[s] = rows
-        wide = rows.astype(F32)
-        squares = squares + wide * wide
-    out_ref[:, logits : logits + 1] = jnp.sum(squares, axis=1, keepdims=True)
+        streams_ref[s] = wide_ref[:, s, :]
+    rows = wide_ref[...].reshape(tokens * streams, width)
+    wide = rows.astype(F32)
+    squares = jnp.sum(wide * wide, axis=1, keepdims=True)
     copies[1].wait()
-    total = jnp.zeros((tokens, logits), F32)
-    for s in range(streams):
-        total = total + nt(streams_ref[s], weight_ref[:, s, :])
-    out_ref[:, :logits] = total
+    pairs = nt(rows, weight_ref[...].reshape(logits * streams, width))
+    token = lax.broadcasted_iota(jnp.int32, pairs.shape, 0)
+    logit = lax.broadcasted_iota(jnp.int32, pairs.shape, 1)
+    pairs = jnp.where(token % streams == logit % streams, pairs, 0.0)
+    by_token = jnp.dot(
+        group(tokens, streams),
+        jnp.concatenate([pairs, squares], axis=1),
+        preferred_element_type=F32,
+        precision=lax.Precision.HIGHEST,
+    )
+    out_ref[:, :logits] = nt(
+        by_token[:, : logits * streams], group(logits, streams), lax.Precision.HIGHEST
+    )
+    out_ref[:, logits : logits + 1] = by_token[:, logits * streams :]
     copies[2].wait()
 
 
-def mix_body(partial_ref, bias_ref, streams_ref, logits_ref, rows_ref):
+def mix_body(bias_ref, streams_ref, *refs):
+    *part_refs, logits_ref, rows_ref = refs
     streams, tokens, width = streams_ref.shape
     count = bias_ref.shape[1]
-    total = jnp.sum(partial_ref[...], axis=0)
+    total = functools.reduce(jnp.add, [ref[...] for ref in part_refs])
     scale = lax.rsqrt(total[:, count : count + 1] / (streams * D) + EPSILON)
     logits = total[:, :count] * scale + bias_ref[...]
     logits_ref[:, :count] = logits
@@ -125,43 +141,54 @@
     out_ref[...] = jnp.concatenate([post] + rows + [spare], axis=0).T
 
 
-def load_body(after_ref, weight_ref, out_ref, sems):
-    count = sems.shape[0]
-    rows = weight_ref.shape[0] // count
+def load_body(after_ref, *refs, spans):
+    n = len(spans)
+    weights, outs, sems = refs[:n], refs[-1 - n : -1], refs[-1]
     copies = []
-    for k in range(count):
-        at = pl.ds(k * rows, rows)
-        copies.append(pltpu.make_async_copy(weight_ref.at[at], out_ref.at[at], sems.at[k]))
+    for weight, out, (first, last) in zip(weights, outs, spans):
+        count = 1 if (last - first) % (16 * COPIES) else COPIES
+        rows = (last - first) // count
+        for k in range(count):
+            at = pl.ds(first + k * rows, rows)
+            sem = sems.at[len(copies)]
+            copies.append(pltpu.make_async_copy(weight.at[at], out.at[at], sem))
     for copy in copies:
         copy.start()
     for copy in copies:
         copy.wait()
 
 
-def load(weight, after):
-    copies = 1 if weight.shape[0] % (16 * COPIES) else COPIES
+def load(after, *jobs):
+    spans = [tuple(weight.shape[0] * x // 6 for x in part) for weight, _, *part in jobs]
+    earlier = [e for _, e, *_ in jobs if e is not None]
+    aliases, at = {}, 1 + len(jobs)
+    for k, (_, e, *_) in enumerate(jobs):
+        if e is not None:
+            aliases[at] = k
+            at += 1
     return call(
-        load_body,
-        jax.ShapeDtypeStruct(weight.shape, weight.dtype),
-        [IN_ANY, IN_HBM],
-        flops=int(3e9),
+        functools.partial(load_body, spans=spans),
+        tuple(jax.ShapeDtypeStruct(weight.shape, weight.dtype) for weight, *_ in jobs),
+        [IN_ANY] + [IN_HBM] * len(jobs) + [IN_VMEM] * len(earlier),
+        flops=int(2e9),
         limit=1 << 20,
-        scratch=[pltpu.SemaphoreType.DMA((copies,))],
-    )(after, in_hbm(weight))
-
-
-def expand_body(after_ref, x_ref, gate_ref, up_ref, send_ref, keep_ref, *, start):
+        aliases=aliases,
+        scratch=[pltpu.SemaphoreType.DMA((COPIES * len(jobs),))],
+    )(after, *[in_hbm(weight) for weight, *_ in jobs], *earlier)
+
+
+def expand_body(after_ref, x_ref, gate_ref, up_ref, send_ref, keep_ref, *, at):
     low = lax.axis_index("tensor") % 2
     size = send_ref.shape[2]
     half = gate_ref.shape[0] // 2
     x = x_ref[...]
     for own, out in ((1 - low, send_ref), (low, keep_ref)):
-        at = pl.ds(pl.multiple_of(own * half + start, 8), size)
-        out[0] = nt(x, gate_ref[at, :]).astype(out.dtype)
-        out[1] = nt(x, up_ref[at, :]).astype(out.dtype)
-
-
-def add_body(keep_ref, got_ref, *refs):
+        units = pl.ds(pl.multiple_of(own * half + at * size, 8), size)
+        out[0] = nt(x, gate_ref[units, :]).astype(out.dtype)
+        out[1] = nt(x, up_ref[units, :]).astype(out.dtype)
+
+
+def part_body(keep_ref, got_ref, *refs):
     before, (sum_far, sent_far, sum_near, sent_near) = refs[:-4], refs[-4:]
     tokens = sum_far.shape[1]
     done = sum_near.shape[2] - keep_ref.shape[2]
@@ -187,19 +214,21 @@
         at += size
 
 
-def reduce_body(after_ref, mine_ref, other_ref, down_ref, *outs):
-    low = lax.axis_index("tensor") % 2
+def own_body(mine_ref, down_ref, out_ref):
     half = down_ref.shape[0] // 2
-    total = None
-    for own, rows in ((low, mine_ref), (1 - low, other_ref)):
-        at = pl.ds(pl.multiple_of(own * half, 8), half)
-        part = jnp.dot(rows[...], down_ref[at, :], preferred_element_type=F32)
-        total = part if total is None else total + part
-    at = 0
+    at = pl.ds(pl.multiple_of(lax.axis_index("tensor") % 2 * half, 8), half)
+    out_ref[...] = jnp.dot(mine_ref[...], down_ref[at, :], preferred_element_type=F32)
+
+
+def other_body(own_ref, other_ref, down_ref, *outs):
+    half = down_ref.shape[0] // 2
+    at = pl.ds(pl.multiple_of((1 - lax.axis_index("tensor") % 2) * half, 8), half)
+    total = own_ref[...] + jnp.dot(other_ref[...], down_ref[at, :], preferred_element_type=F32)
+    row = 0
     for out_ref in outs:
         size = out_ref.shape[0]
-        out_ref[...] = total[at : at + size].astype(out_ref.dtype)
-        at += size
+        out_ref[...] = total[row : row + size].astype(out_ref.dtype)
+        row += size
 
 
 def pieces_of(half):
@@ -227,16 +256,17 @@
             pltpu.SemaphoreType.DMA((3,)),
         ],
     )(in_hbm(streams), in_hbm(mix_weight), in_hbm(mix_bias[None, :]))
-    gathered = lax.all_gather(partial, "tensor")
+    parts = [partial] + [flip(partial, "tensor", k) for k in range(1, lax.axis_size("tensor"))]
+    (gate,) = load(partial, (gate_weight, None, 0, 2))
     logits, rows = call(
         mix_body,
         (shape((tokens, LANES), F32), shape((tokens, width), BF16)),
-        [IN_VMEM] * 3,
-    )(gathered, bias, turned)
-
-    gate = load(gate_weight, rows)
+        [IN_VMEM] * (2 + len(parts)),
+    )(bias, turned, *parts)
+
+    (gate,) = load(rows, (gate_weight, gate, 2, 6))
     rows, near_rows = gather_tokens(rows)
-    up = load(up_weight, near_rows)
+    up, down = load(near_rows, (up_weight, None, 0, 6), (down_weight, None, 0, 2))
     every = rows.shape[0]
     part = every // 2
     tensor_size = lax.axis_size("tensor")
@@ -251,17 +281,18 @@
         return total, flip(sent, "tensor", bit)
 
     far, before = [], ()
-    afters = [rows]
+    after = rows
     for at, (start, size) in enumerate(pieces):
         send, keep = call(
-            functools.partial(expand_body, start=start),
+            functools.partial(expand_body, at=at),
             (shape((2, every, size), BF16), shape((2, every, size), F32)),
             [IN_ANY] + [IN_VMEM] * 3,
             flops=8 * every * size * width,
-        )(afters[max(0, at - 1)], rows, gate, up)
+        )(after, rows, gate, up)
         got = flip(send, "tensor", 1)
+        after = send
         far_sum, far_sent, *before = call(
-            add_body,
+            part_body,
             (
                 shape((2, part, size), F32),
                 shape((2, part, size), BF16),
@@ -270,44 +301,42 @@
             ),
             [IN_VMEM] * (2 + len(before)),
         )(keep, got, *before)
-        afters.append(far_sent)
         far.append(across(far_sum, far_sent))
-    near = across(*before)
-    down = load(down_weight, before[1])
+    near = [across(*before)]
+    (down,) = load(before[1], (down_weight, down, 2, 6))
+    half = gate_weight.shape[0] // 2
 
     def outward(pairs, after, outs):
         mine = call(
             hidden_body,
-            shape((part, gate_weight.shape[0] // 2), BF16),
+            shape((part, half), BF16),
             [IN_ANY] + [IN_VMEM] * (2 * len(pairs)),
         )(after, *[x for pair in pairs for x in pair])
         other = flip(mine, "tensor", 1)
-        return call(
-            reduce_body,
-            outs,
-            [IN_ANY] + [IN_VMEM] * 3,
-            flops=4 * part * gate_weight.shape[0] * width,
-        )(after, mine, other, down)
+        flops = 2 * part * half * width
+        own = call(own_body, shape((part, width), F32), [IN_VMEM] * 2, flops=flops)(mine, down)
+        return call(other_body, outs, [IN_VMEM] * 3, flops=flops)(own, other, down)
 
     step = every // 4
-    sent = [shape((step, width), BF16)] * 2
-    two, three = outward(far, before[1], sent)
+    sent = shape((step, width), BF16)
+    two, three = outward(far, before[1], [sent, sent])
     got = [flip(two, "dp", 2), flip(three, "dp", 3)]
-    kept, one = outward([near], two, [shape((step, width), F32), sent[0]])
+    kept, one = outward(near, two, [shape((step, width), F32), sent])
     got.append(flip(one, "dp", 1))
-    mlp_out = scatter_tokens(kept, got)
     mixing = call(
         functools.partial(sinkhorn_body, streams=stream_count),
         shape((tokens, LANES), F32),
         [IN_ANY, IN_VMEM],
         flops=int(1e9),
-    )(kept, logits)
+    )(one, logits)
     post_gate = mixing[:, :stream_count]
     entries = mixing[:, stream_count : stream_count + stream_count**2]
     res_mix = entries.reshape(tokens, stream_count, stream_count)
     mixed = jnp.einsum(
         "tij,tjc->tic", res_mix, streams.astype(F32), precision=lax.Precision.HIGHEST
     )
+    mixed, post_gate = lax.optimization_barrier((mixed, post_gate))
+    mlp_out = scatter_tokens(kept, got)
     mixed = mixed + post_gate[:, :, None] * mlp_out[:, None, :]
     return mixed.astype(BF16)
 

time: 64.8 us -> 62.1 us (0.958)
  blocking collectives: 6.23 us -> 0 us
  starting transfers between devices: 17.9 us -> 21.6 us
  other arithmetic: 0.07 us -> 0.94 us
  matrix products: 1.22 us -> 0.51 us
    all_gather x1 -> x0, blocking collectives: 6.23 us -> none  [layer(): gathered = lax.all_gather(partial, 'tensor')]
    ppermute x17 -> x20, starting transfers between devices: 17.9 us -> 21.6 us  [flip(): return lax.ppermute(value, axis, [(i, i ^ bits) for i in range(size)])]
    convert_element_type x0 -> x1, other arithmetic: none -> 0.87 us  [layer(): return mixed.astype(BF16)]
    dot_general x1, matrix products: 1.22 us -> 0.51 us  [layer(): jnp.einsum('tij,tjc->tic', res_mix, streams.astype(F32), precision=lax.Pr...]
    ppermute x17 -> x20, waiting for transfers between devices: 16.7 us -> 16.2 us  [flip(): return lax.ppermute(value, axis, [(i, i ^ bits) for i in range(size)])]
    pallas_call x13 -> x16, Pallas kernels: 18.8 us -> 19.2 us  [the longest x4 11.2 us: load(): call(functools.partial(load_body, spans=spans), tuple((jax.ShapeDtypeStru...]
  transfers between devices with their start and end apart: 17 -> 20, of which waited for: 8 -> 9; matrix products, arithmetic and copies ran while one was open for 0% -> 1% of each run, Pallas kernels for 27% -> 29%
where the time goes in v2:
time: 62.1 us; the launch traced here: 62 us
  Pallas kernels  22.2 us (36%)
  starting transfers between devices  21.6 us (35%)
  waiting for transfers between devices  16.2 us (26%)
  other arithmetic  0.94 us (2%)
    ppermute x20, starting transfers between devices, flip(): return lax.ppermute(value, axis, [(i, i ^ bits) for i in range(size)])  21.6 us
    ppermute x20, waiting for transfers between devices, flip(): return lax.ppermute(value, axis, [(i, i ^ bits) for i in range(size)])  16.2 us
    pallas_call x4, Pallas kernels, load(): call(functools.partial(load_body, spans=spans), tuple((jax.ShapeDtypeStru...  11.2 us
    pallas_call x3, Pallas kernels, layer(): call(functools.partial(expand_body, at=at), (shape((2, every, size), BF16...  4.87 us
    pallas_call x1, Pallas kernels, layer(): call(logits_body, (shape((tokens, LANES), F32), shape((stream_count, toke...  2.09 us
    pallas_call x2, Pallas kernels, outward(): return call(other_body, outs, [IN_VMEM] * 3, flops=flops)(own, other, down)  1.42 us
    pallas_call x2, Pallas kernels, outward(): call(own_body, shape((part, width), F32), [IN_VMEM] * 2, flops=flops)  1.39 us
  transfers between devices with their start and end apart: 20, of which 9 were waited for; matrix products, arithmetic and copies ran while one was open for 1% of the time, Pallas kernels for 29%

profile of v2, /device:TPU:0, one launch (start us, length us, event | category | flops | bytes accessed | tf_op | source)
XLA Modules:
  0.0 62.0 jit_solution(129622852196533409)
XLA Ops:
  0.0 2.1 %shard_map.64 = (f32[16,128]{1,0:T(8,128)S(1)}, bf16[4,16,1792]{2,1,0:T(8,128)(2,1)S(1)}, f32[1,24]{1,0:T(1,128)S(1)}) custom-call(bf16[16,4,1792]{2,1,0:T(4,128)(2,1)} %streams_hbm.1, bf16[24,4,1792]{2,1,0:T(4,128)(2,1)} %weight_hbm.1, f32[1,24]{1,0:T(1,128)} %bitcast.7), custom_call_target="tpu_custom_call" | custom-call | tf_op jit(solution)/shard_map/pallas_call | solution.py:245
  2.1 2.5 %collective-permute-start.2 = (f32[16,128]{1,0:T(8,128)S(1)}, f32[16,128]{1,0:T(8,128)S(1)}, u32[]{:S(2)}, u32[]{:S(2)}) collective-permute-start(f32[16,128]{1,0:T(8,128)S(1)} %get-tuple-element.38.refs_0_.after_ref), channel_id=1, source_target_pairs={{0,3},{1,2},{2,1},{3,0},{4,7},{5,6},{6,5},{7,4},{8,11},{9,10},{10,... | collective-permute-start | bytes 24584 | tf_op jit(solution)/shard_map/ppermute | solution.py:45
  5.3 1.8 %shard_map.66.refs_1_ = bf16[2304,1792]{1,0:T(8,128)(2,1)S(1)} custom-call(f32[16,128]{1,0:T(8,128)S(1)} %get-tuple-element.38.refs_0_.after_ref, bf16[2304,1792]{1,0:T(8,128)(2,1)} %refs_0_.5), custom_call_target="tpu_custom_call" | custom-call | flops 2000000000 | tf_op jit(solution)/shard_map/pallas_call | solution.py:169
  7.1 1.2 %collective-permute-done.1.refs_2_ = f32[16,128]{1,0:T(8,128)S(1)} collective-permute-done((f32[16,128]{1,0:T(8,128)S(1)}, f32[16,128]{1,0:T(8,128)S(1)}, u32[]{:S(2)}, u32[]{:S(2)}) %collective-permute-start.1) | collective-permute-done | bytes 8224 | tf_op jit(solution)/shard_map/ppermute | solution.py:45
  8.5 2.7 %collective-permute-start.3 = (bf16[16,1792]{1,0:T(8,128)(2,1)S(1)}, bf16[16,1792]{1,0:T(8,128)(2,1)S(1)}, u32[]{:S(2)}, u32[]{:S(2)}) collective-permute-start(bf16[16,1792]{1,0:T(8,128)(2,1)S(1)} %get-tuple-element.39.after_ref), channel_id=1, source_target_pairs={{0,16},{4,20},{8,24},{12,28},{16,0},{20,4},{24,8},{28,12},{1,17},{... | collective-permute-start | bytes 172040 | tf_op jit(solution)/shard_map/ppermute | solution.py:45
  11.1 2.6 %shard_map.67.gate_ref = bf16[2304,1792]{1,0:T(8,128)(2,1)S(1)} custom-call(bf16[16,1792]{1,0:T(8,128)(2,1)S(1)} %get-tuple-element.39.after_ref, bf16[2304,1792]{1,0:T(8,128)(2,1)} %refs_0_.5, bf16[2304,1792]{1,0:T(8,128)(2,1)S(1)} %shard_map.66.refs_1_), custom_call_target="tpu_custom_call", output_to_operand_aliasing={{}: (2, {})} | custom-call | flops 2000000000 | tf_op jit(solution)/shard_map/pallas_call | solution.py:169
  13.8 2.6 %collective-permute-start.6 = (bf16[32,1792]{1,0:T(8,128)(2,1)S(1)}, bf16[32,1792]{1,0:T(8,128)(2,1)S(1)}, u32[]{:S(2)}, u32[]{:S(2)}) collective-permute-start(bf16[32,1792]{1,0:T(8,128)(2,1)S(1)} %get-tuple-element.67.after_ref), channel_id=1, source_target_pairs={{0,12},{4,8},{8,4},{12,0},{16,28},{20,24},{24,20},{28,16},{1,13},{... | collective-permute-start | bytes 344072 | tf_op jit(solution)/shard_map/ppermute | solution.py:45
  17.4 4.2 %shard_map.68 = (bf16[2304,1792]{1,0:T(8,128)(2,1)S(1)}, bf16[2304,1792]{1,0:T(8,128)(2,1)S(1)}) custom-call(bf16[32,1792]{1,0:T(8,128)(2,1)S(1)} %get-tuple-element.67.after_ref, bf16[2304,1792]{1,0:T(8,128)(2,1)} %refs_0_.6, bf16[2304,1792]{1,0:T(8,128)(2,1)} %refs_0_.7), custom_call_target="tpu_custom_call" | custom-call | flops 2000000000 | tf_op jit(solution)/shard_map/pallas_call | solution.py:169
  21.8 1.6 %shard_map.69 = (bf16[2,128,384]{2,1,0:T(8,128)(2,1)S(1)}, f32[2,128,384]{2,1,0:T(8,128)S(1)}) custom-call(bf16[128,1792]{1,0:T(8,128)(2,1)S(1)} %constant_dynamic-update-slice_fusion.2.after_ref.x_ref, bf16[128,1792]{1,0:T(8,128)(2,1)S(1)} %constant_dynamic-update-slice_fusion.2.after_ref.x_ref, bf16[2304,1792]{1,0:T(8,128)(2,1)S(1)} %shard_map.67.gate_ref, ...), custom_call_target="tpu_custom_call" | custom-call | flops 704643072 | tf_op jit(solution)/shard_map/pallas_call | solution.py:286
  23.6 1.6 %shard_map.70 = (bf16[2,128,384]{2,1,0:T(8,128)(2,1)S(1)}, f32[2,128,384]{2,1,0:T(8,128)S(1)}) custom-call(bf16[2,128,384]{2,1,0:T(8,128)(2,1)S(1)} %get-tuple-element.41.after_ref, bf16[128,1792]{1,0:T(8,128)(2,1)S(1)} %constant_dynamic-update-slice_fusion.2.after_ref.x_ref, bf16[2304,1792]{1,0:T(8,128)(2,1)S(1)} %shard_map.67.gate_ref, ...), custom_call_target="tpu_custom_call" | custom-call | flops 704643072 | tf_op jit(solution)/shard_map/pallas_call | solution.py:286
  25.7 1.6 %shard_map.71 = (bf16[2,128,384]{2,1,0:T(8,128)(2,1)S(1)}, f32[2,128,384]{2,1,0:T(8,128)S(1)}) custom-call(bf16[2,128,384]{2,1,0:T(8,128)(2,1)S(1)} %get-tuple-element.42.after_ref, bf16[128,1792]{1,0:T(8,128)(2,1)S(1)} %constant_dynamic-update-slice_fusion.2.after_ref.x_ref, bf16[2304,1792]{1,0:T(8,128)(2,1)S(1)} %shard_map.67.gate_ref, ...), custom_call_target="tpu_custom_call" | custom-call | flops 704643072 | tf_op jit(solution)/shard_map/pallas_call | solution.py:286
  27.5 1.6 %collective-permute-start.10 = (bf16[2,64,384]{2,1,0:T(8,128)(2,1)S(1)}, bf16[2,64,384]{2,1,0:T(8,128)(2,1)S(1)}, u32[]{:S(2)}, u32[]{:S(2)}) collective-permute-start(bf16[2,64,384]{2,1,0:T(8,128)(2,1)S(1)} %get-tuple-element.53), channel_id=1, source_target_pairs={{0,2},{1,3},{2,0},{3,1},{4,6},{5,7},{6,4},{7,5},{8,10},{9,11},{10,... | collective-permute-start | bytes 294920 | tf_op jit(solution)/shard_map/ppermute | solution.py:45
  29.3 1.3 %collective-permute-start.12 = (bf16[2,64,384]{2,1,0:T(8,128)(2,1)S(1)}, bf16[2,64,384]{2,1,0:T(8,128)(2,1)S(1)}, u32[]{:S(2)}, u32[]{:S(2)}) collective-permute-start(bf16[2,64,384]{2,1,0:T(8,128)(2,1)S(1)} %get-tuple-element.57), channel_id=1, source_target_pairs={{0,2},{1,3},{2,0},{3,1},{4,6},{5,7},{6,4},{7,5},{8,10},{9,11},{10,... | collective-permute-start | bytes 294920 | tf_op jit(solution)/shard_map/ppermute | solution.py:45
  30.5 0.8 %collective-permute-start.11 = (bf16[2,64,384]{2,1,0:T(8,128)(2,1)S(1)}, bf16[2,64,384]{2,1,0:T(8,128)(2,1)S(1)}, u32[]{:S(2)}, u32[]{:S(2)}) collective-permute-start(bf16[2,64,384]{2,1,0:T(8,128)(2,1)S(1)} %get-tuple-element.55), channel_id=1, source_target_pairs={{0,2},{1,3},{2,0},{3,1},{4,6},{5,7},{6,4},{7,5},{8,10},{9,11},{10,... | collective-permute-start | bytes 294920 | tf_op jit(solution)/shard_map/ppermute | solution.py:45
  31.4 1.2 %collective-permute-start.14 = (bf16[2,64,1152]{2,1,0:T(8,128)(2,1)S(1)}, bf16[2,64,1152]{2,1,0:T(8,128)(2,1)S(1)}, u32[]{:S(2)}, u32[]{:S(2)}) collective-permute-start(bf16[2,64,1152]{2,1,0:T(8,128)(2,1)S(1)} %get-tuple-element.51.after_ref), channel_id=1, source_target_pairs={{0,2},{1,3},{2,0},{3,1},{4,6},{5,7},{6,4},{7,5},{8,10},{9,11},{10,... | collective-permute-start | bytes 884744 | tf_op jit(solution)/shard_map/ppermute | solution.py:45
  32.6 0.7 %collective-permute-done.10.refs_1_ = bf16[2,64,384]{2,1,0:T(8,128)(2,1)S(1)} collective-permute-done((bf16[2,64,384]{2,1,0:T(8,128)(2,1)S(1)}, bf16[2,64,384]{2,1,0:T(8,128)(2,1)S(1)}, u32[]{:S(2)}, u32[]{:S(2)}) %collective-permute-start.10) | collective-permute-done | bytes 98336 | tf_op jit(solution)/shard_map/ppermute | solution.py:45
  33.2 2.1 %collective-permute-done.12.refs_5_ = bf16[2,64,384]{2,1,0:T(8,128)(2,1)S(1)} collective-permute-done((bf16[2,64,384]{2,1,0:T(8,128)(2,1)S(1)}, bf16[2,64,384]{2,1,0:T(8,128)(2,1)S(1)}, u32[]{:S(2)}, u32[]{:S(2)}) %collective-permute-start.12) | collective-permute-done | bytes 98336 | tf_op jit(solution)/shard_map/ppermute | solution.py:45
  35.3 2.1 %collective-permute-done.11.refs_3_ = bf16[2,64,384]{2,1,0:T(8,128)(2,1)S(1)} collective-permute-done((bf16[2,64,384]{2,1,0:T(8,128)(2,1)S(1)}, bf16[2,64,384]{2,1,0:T(8,128)(2,1)S(1)}, u32[]{:S(2)}, u32[]{:S(2)}) %collective-permute-start.11) | collective-permute-done | bytes 98336 | tf_op jit(solution)/shard_map/ppermute | solution.py:45
  37.6 2.6 %shard_map.76.down_ref = bf16[2304,1792]{1,0:T(8,128)(2,1)S(1)} custom-call(bf16[2,64,1152]{2,1,0:T(8,128)(2,1)S(1)} %get-tuple-element.51.after_ref, bf16[2304,1792]{1,0:T(8,128)(2,1)} %refs_0_.7, bf16[2304,1792]{1,0:T(8,128)(2,1)S(1)} %get-tuple-element.58.refs_1_), custom_call_target="tpu_custom_call", output_to_operand_aliasing={{}: (2, {})} | custom-call | flops 2000000000 | tf_op jit(solution)/shard_map/pallas_call | solution.py:169
  40.3 0.7 %shard_map.77.own_ref = f32[64,1792]{1,0:T(8,128)S(1)} custom-call(bf16[64,1152]{1,0:T(8,128)(2,1)S(1)} %shard_map.75.mine_ref, bf16[2304,1792]{1,0:T(8,128)(2,1)S(1)} %shard_map.76.down_ref), custom_call_target="tpu_custom_call" | custom-call | flops 264241152 | tf_op jit(solution)/shard_map/pallas_call | solution.py:317
  41.0 0.7 %shard_map.78 = (bf16[32,1792]{1,0:T(8,128)(2,1)S(1)}, bf16[32,1792]{1,0:T(8,128)(2,1)S(1)}) custom-call(f32[64,1792]{1,0:T(8,128)S(1)} %shard_map.77.own_ref, bf16[64,1152]{1,0:T(8,128)(2,1)S(1)} %collective-permute-done.13.other_ref, bf16[2304,1792]{1,0:T(8,128)(2,1)S(1)} %shard_map.76.down_ref), custom_call_target="tpu_custom_call" | custom-call | flops 264241152 | tf_op jit(solution)/shard_map/pallas_call | solution.py:318
  41.7 1.6 %collective-permute-done.14.refs_1_ = bf16[2,64,1152]{2,1,0:T(8,128)(2,1)S(1)} collective-permute-done((bf16[2,64,1152]{2,1,0:T(8,128)(2,1)S(1)}, bf16[2,64,1152]{2,1,0:T(8,128)(2,1)S(1)}, u32[]{:S(2)}, u32[]{:S(2)}) %collective-permute-start.14) | collective-permute-done | bytes 294944 | tf_op jit(solution)/shard_map/ppermute | solution.py:45
  43.5 1.6 %collective-permute-start.16 = (bf16[32,1792]{1,0:T(8,128)(2,1)S(1)}, bf16[32,1792]{1,0:T(8,128)(2,1)S(1)}, u32[]{:S(2)}, u32[]{:S(2)}) collective-permute-start(bf16[32,1792]{1,0:T(8,128)(2,1)S(1)} %get-tuple-element.59.after_ref), channel_id=1, source_target_pairs={{0,8},{4,12},{8,0},{12,4},{16,24},{20,28},{24,16},{28,20},{1,9},{5... | collective-permute-start | bytes 344072 | tf_op jit(solution)/shard_map/ppermute | solution.py:45
  45.1 1.2 %collective-permute-start.17 = (bf16[32,1792]{1,0:T(8,128)(2,1)S(1)}, bf16[32,1792]{1,0:T(8,128)(2,1)S(1)}, u32[]{:S(2)}, u32[]{:S(2)}) collective-permute-start(bf16[32,1792]{1,0:T(8,128)(2,1)S(1)} %get-tuple-element.66), channel_id=1, source_target_pairs={{0,12},{4,8},{8,4},{12,0},{16,28},{20,24},{24,20},{28,16},{1,13},{... | collective-permute-start | bytes 344072 | tf_op jit(solution)/shard_map/ppermute | solution.py:45
  46.3 0.7 %shard_map.80.own_ref = f32[64,1792]{1,0:T(8,128)S(1)} custom-call(bf16[64,1152]{1,0:T(8,128)(2,1)S(1)} %shard_map.79.mine_ref, bf16[2304,1792]{1,0:T(8,128)(2,1)S(1)} %shard_map.76.down_ref), custom_call_target="tpu_custom_call" | custom-call | flops 264241152 | tf_op jit(solution)/shard_map/pallas_call | solution.py:317
  47.0 0.7 %shard_map.81 = (f32[32,1792]{1,0:T(8,128)S(1)}, bf16[32,1792]{1,0:T(8,128)(2,1)S(1)}) custom-call(f32[64,1792]{1,0:T(8,128)S(1)} %shard_map.80.own_ref, bf16[64,1152]{1,0:T(8,128)(2,1)S(1)} %collective-permute-done.15.other_ref, bf16[2304,1792]{1,0:T(8,128)(2,1)S(1)} %shard_map.76.down_ref), custom_call_target="tpu_custom_call" | custom-call | flops 264241152 | tf_op jit(solution)/shard_map/pallas_call | solution.py:318
  47.7 0.8 %collective-permute-start.18 = (bf16[32,1792]{1,0:T(8,128)(2,1)S(1)}, bf16[32,1792]{1,0:T(8,128)(2,1)S(1)}, u32[]{:S(2)}, u32[]{:S(2)}) collective-permute-start(bf16[32,1792]{1,0:T(8,128)(2,1)S(1)} %get-tuple-element.61.after_ref), channel_id=1, source_target_pairs={{0,4},{4,0},{8,12},{12,8},{16,20},{20,16},{24,28},{28,24},{1,5},{5... | collective-permute-start | bytes 344072 | tf_op jit(solution)/shard_map/ppermute | solution.py:45
  49.4 2.8 %collective-permute-done.17 = bf16[32,1792]{1,0:T(8,128)(2,1)S(1)} collective-permute-done((bf16[32,1792]{1,0:T(8,128)(2,1)S(1)}, bf16[32,1792]{1,0:T(8,128)(2,1)S(1)}, u32[]{:S(2)}, u32[]{:S(2)}) %collective-permute-start.17) | collective-permute-done | bytes 114720 | tf_op jit(solution)/shard_map/ppermute | solution.py:45
  52.3 2.3 %collective-permute-done.18 = bf16[32,1792]{1,0:T(8,128)(2,1)S(1)} collective-permute-done((bf16[32,1792]{1,0:T(8,128)(2,1)S(1)}, bf16[32,1792]{1,0:T(8,128)(2,1)S(1)}, u32[]{:S(2)}, u32[]{:S(2)}) %collective-permute-start.18) | collective-permute-done | bytes 114720 | tf_op jit(solution)/shard_map/ppermute | solution.py:45
  54.7 2.8 %collective-permute-start.19 = (bf16[16,1792]{1,0:T(8,128)(2,1)S(1)}, bf16[16,1792]{1,0:T(8,128)(2,1)S(1)}, u32[]{:S(2)}, u32[]{:S(2)}) collective-permute-start(bf16[16,1792]{1,0:T(8,128)(2,1)S(1)} %slice.23), channel_id=1, source_target_pairs={{0,16},{4,20},{8,24},{12,28},{16,0},{20,4},{24,8},{28,12},{1,17},{... | collective-permute-start | bytes 172040 | tf_op jit(solution)/shard_map/ppermute | solution.py:45
  58.0 3.0 %collective-permute-done.19 = bf16[16,1792]{1,0:T(8,128)(2,1)S(1)} collective-permute-done((bf16[16,1792]{1,0:T(8,128)(2,1)S(1)}, bf16[16,1792]{1,0:T(8,128)(2,1)S(1)}, u32[]{:S(2)}, u32[]{:S(2)}) %collective-permute-start.19) | collective-permute-done | bytes 57376 | tf_op jit(solution)/shard_map/ppermute | solution.py:45
  61.1 0.9 %add_convert_fusion = bf16[16,4,1792]{2,1,0:T(4,128)(2,1)} fusion(f32[16,4,1792]{2,1,0:T(4,128)S(1)} %fusion, f32[16,1792]{1,0:T(8,128)S(1)} %slice_add_fusion, f32[16,4]{1,0:T(8,128)S(1)} %bitcast.5), kind=kLoop, calls=%fused_computation | loop fusion | flops 344064 | bytes 803072 | tf_op jit(solution)/shard_map/convert_element_type | solution.py:341
  (42 shorter events, 5.0 us)
Async XLA Ops:
  2.1 4.9 %collective-permute-start.2 = (f32[16,128]{1,0:T(8,128)S(1)}, f32[16,128]{1,0:T(8,128)S(1)}, u32[]{:S(2)}, u32[]{:S(2)}) collective-permute-start(f32[16,128]{1,0:T(8,128)S(1)} %get-tuple-element.38.refs_0_.after_ref), channel_id=1, source_target_pairs={{0,3},{1,2},{2,1},{3,0},{4,7},{5,6},{6,5},{7,4},{8,11},{9,10},{10,... | collective-permute-start | bytes 24584 | tf_op jit(solution)/shard_map/ppermute | solution.py:45
  4.6 3.7 %collective-permute-start.1 = (f32[16,128]{1,0:T(8,128)S(1)}, f32[16,128]{1,0:T(8,128)S(1)}, u32[]{:S(2)}, u32[]{:S(2)}) collective-permute-start(f32[16,128]{1,0:T(8,128)S(1)} %get-tuple-element.38.refs_0_.after_ref), channel_id=1, source_target_pairs={{0,2},{1,3},{2,0},{3,1},{4,6},{5,7},{6,4},{7,5},{8,10},{9,11},{10,... | collective-permute-start | bytes 24584 | tf_op jit(solution)/shard_map/ppermute | solution.py:45
  5.2 3.0 %collective-permute-start = (f32[16,128]{1,0:T(8,128)S(1)}, f32[16,128]{1,0:T(8,128)S(1)}, u32[]{:S(2)}, u32[]{:S(2)}) collective-permute-start(f32[16,128]{1,0:T(8,128)S(1)} %get-tuple-element.38.refs_0_.after_ref), channel_id=1, source_target_pairs={{0,1},{1,0},{2,3},{3,2},{4,5},{5,4},{6,7},{7,6},{8,9},{9,8},{10,11... | collective-permute-start | bytes 24584 | tf_op jit(solution)/shard_map/ppermute | solution.py:45
  8.5 5.3 %collective-permute-start.3 = (bf16[16,1792]{1,0:T(8,128)(2,1)S(1)}, bf16[16,1792]{1,0:T(8,128)(2,1)S(1)}, u32[]{:S(2)}, u32[]{:S(2)}) collective-permute-start(bf16[16,1792]{1,0:T(8,128)(2,1)S(1)} %get-tuple-element.39.after_ref), channel_id=1, source_target_pairs={{0,16},{4,20},{8,24},{12,28},{16,0},{20,4},{24,8},{28,12},{1,17},{... | collective-permute-start | bytes 172040 | tf_op jit(solution)/shard_map/ppermute | solution.py:45
  13.8 8.0 %collective-permute-start.6 = (bf16[32,1792]{1,0:T(8,128)(2,1)S(1)}, bf16[32,1792]{1,0:T(8,128)(2,1)S(1)}, u32[]{:S(2)}, u32[]{:S(2)}) collective-permute-start(bf16[32,1792]{1,0:T(8,128)(2,1)S(1)} %get-tuple-element.67.after_ref), channel_id=1, source_target_pairs={{0,12},{4,8},{8,4},{12,0},{16,28},{20,24},{24,20},{28,16},{1,13},{... | collective-permute-start | bytes 344072 | tf_op jit(solution)/shard_map/ppermute | solution.py:45
  16.4 5.4 %collective-permute-start.5 = (bf16[32,1792]{1,0:T(8,128)(2,1)S(1)}, bf16[32,1792]{1,0:T(8,128)(2,1)S(1)}, u32[]{:S(2)}, u32[]{:S(2)}) collective-permute-start(bf16[32,1792]{1,0:T(8,128)(2,1)S(1)} %get-tuple-element.67.after_ref), channel_id=1, source_target_pairs={{0,8},{4,12},{8,0},{12,4},{16,24},{20,28},{24,16},{28,20},{1,9},{5... | collective-permute-start | bytes 344072 | tf_op jit(solution)/shard_map/ppermute | solution.py:45
  16.8 5.0 %collective-permute-start.4 = (bf16[32,1792]{1,0:T(8,128)(2,1)S(1)}, bf16[32,1792]{1,0:T(8,128)(2,1)S(1)}, u32[]{:S(2)}, u32[]{:S(2)}) collective-permute-start(bf16[32,1792]{1,0:T(8,128)(2,1)S(1)} %get-tuple-element.67.after_ref), channel_id=1, source_target_pairs={{0,4},{4,0},{8,12},{12,8},{16,20},{20,16},{24,28},{28,24},{1,5},{5... | collective-permute-start | bytes 344072 | tf_op jit(solution)/shard_map/ppermute | solution.py:45
  23.5 4.0 %collective-permute-start.9 = (bf16[2,128,384]{2,1,0:T(8,128)(2,1)S(1)}, bf16[2,128,384]{2,1,0:T(8,128)(2,1)S(1)}, u32[]{:S(2)}, u32[]{:S(2)}) collective-permute-start(bf16[2,128,384]{2,1,0:T(8,128)(2,1)S(1)} %get-tuple-element.41.after_ref), channel_id=1, source_target_pairs={{0,1},{1,0},{2,3},{3,2},{4,5},{5,4},{6,7},{7,6},{8,9},{9,8},{10,11... | collective-permute-start | bytes 589832 | tf_op jit(solution)/shard_map/ppermute | solution.py:45
  25.2 3.9 %collective-permute-start.8 = (bf16[2,128,384]{2,1,0:T(8,128)(2,1)S(1)}, bf16[2,128,384]{2,1,0:T(8,128)(2,1)S(1)}, u32[]{:S(2)}, u32[]{:S(2)}) collective-permute-start(bf16[2,128,384]{2,1,0:T(8,128)(2,1)S(1)} %get-tuple-element.42.after_ref), channel_id=1, source_target_pairs={{0,1},{1,0},{2,3},{3,2},{4,5},{5,4},{6,7},{7,6},{8,9},{9,8},{10,11... | collective-permute-start | bytes 589832 | tf_op jit(solution)/shard_map/ppermute | solution.py:45
  27.3 1.8 %collective-permute-start.7 = (bf16[2,128,384]{2,1,0:T(8,128)(2,1)S(1)}, bf16[2,128,384]{2,1,0:T(8,128)(2,1)S(1)}, u32[]{:S(2)}, u32[]{:S(2)}) collective-permute-start(bf16[2,128,384]{2,1,0:T(8,128)(2,1)S(1)} %get-tuple-element.44), channel_id=1, source_target_pairs={{0,1},{1,0},{2,3},{3,2},{4,5},{5,4},{6,7},{7,6},{8,9},{9,8},{10,11... | collective-permute-start | bytes 589832 | tf_op jit(solution)/shard_map/ppermute | solution.py:45
  27.5 5.7 %collective-permute-start.10 = (bf16[2,64,384]{2,1,0:T(8,128)(2,1)S(1)}, bf16[2,64,384]{2,1,0:T(8,128)(2,1)S(1)}, u32[]{:S(2)}, u32[]{:S(2)}) collective-permute-start(bf16[2,64,384]{2,1,0:T(8,128)(2,1)S(1)} %get-tuple-element.53), channel_id=1, source_target_pairs={{0,2},{1,3},{2,0},{3,1},{4,6},{5,7},{6,4},{7,5},{8,10},{9,11},{10,... | collective-permute-start | bytes 294920 | tf_op jit(solution)/shard_map/ppermute | solution.py:45
  29.3 6.1 %collective-permute-start.12 = (bf16[2,64,384]{2,1,0:T(8,128)(2,1)S(1)}, bf16[2,64,384]{2,1,0:T(8,128)(2,1)S(1)}, u32[]{:S(2)}, u32[]{:S(2)}) collective-permute-start(bf16[2,64,384]{2,1,0:T(8,128)(2,1)S(1)} %get-tuple-element.57), channel_id=1, source_target_pairs={{0,2},{1,3},{2,0},{3,1},{4,6},{5,7},{6,4},{7,5},{8,10},{9,11},{10,... | collective-permute-start | bytes 294920 | tf_op jit(solution)/shard_map/ppermute | solution.py:45
  30.5 6.9 %collective-permute-start.11 = (bf16[2,64,384]{2,1,0:T(8,128)(2,1)S(1)}, bf16[2,64,384]{2,1,0:T(8,128)(2,1)S(1)}, u32[]{:S(2)}, u32[]{:S(2)}) collective-permute-start(bf16[2,64,384]{2,1,0:T(8,128)(2,1)S(1)} %get-tuple-element.55), channel_id=1, source_target_pairs={{0,2},{1,3},{2,0},{3,1},{4,6},{5,7},{6,4},{7,5},{8,10},{9,11},{10,... | collective-permute-start | bytes 294920 | tf_op jit(solution)/shard_map/ppermute | solution.py:45
  31.4 11.9 %collective-permute-start.14 = (bf16[2,64,1152]{2,1,0:T(8,128)(2,1)S(1)}, bf16[2,64,1152]{2,1,0:T(8,128)(2,1)S(1)}, u32[]{:S(2)}, u32[]{:S(2)}) collective-permute-start(bf16[2,64,1152]{2,1,0:T(8,128)(2,1)S(1)} %get-tuple-element.51.after_ref), channel_id=1, source_target_pairs={{0,2},{1,3},{2,0},{3,1},{4,6},{5,7},{6,4},{7,5},{8,10},{9,11},{10,... | collective-permute-start | bytes 884744 | tf_op jit(solution)/shard_map/ppermute | solution.py:45
  37.5 3.4 %collective-permute-start.13 = (bf16[64,1152]{1,0:T(8,128)(2,1)S(1)}, bf16[64,1152]{1,0:T(8,128)(2,1)S(1)}, u32[]{:S(2)}, u32[]{:S(2)}) collective-permute-start(bf16[64,1152]{1,0:T(8,128)(2,1)S(1)} %shard_map.75.mine_ref), channel_id=1, source_target_pairs={{0,1},{1,0},{2,3},{3,2},{4,5},{5,4},{6,7},{7,6},{8,9},{9,8},{10,11... | collective-permute-start | bytes 442376 | tf_op jit(solution)/shard_map/ppermute | solution.py:45
  43.4 3.6 %collective-permute-start.15 = (bf16[64,1152]{1,0:T(8,128)(2,1)S(1)}, bf16[64,1152]{1,0:T(8,128)(2,1)S(1)}, u32[]{:S(2)}, u32[]{:S(2)}) collective-permute-start(bf16[64,1152]{1,0:T(8,128)(2,1)S(1)} %shard_map.79.mine_ref), channel_id=1, source_target_pairs={{0,1},{1,0},{2,3},{3,2},{4,5},{5,4},{6,7},{7,6},{8,9},{9,8},{10,11... | collective-permute-start | bytes 442376 | tf_op jit(solution)/shard_map/ppermute | solution.py:45
  43.5 8.8 %collective-permute-start.16 = (bf16[32,1792]{1,0:T(8,128)(2,1)S(1)}, bf16[32,1792]{1,0:T(8,128)(2,1)S(1)}, u32[]{:S(2)}, u32[]{:S(2)}) collective-permute-start(bf16[32,1792]{1,0:T(8,128)(2,1)S(1)} %get-tuple-element.59.after_ref), channel_id=1, source_target_pairs={{0,8},{4,12},{8,0},{12,4},{16,24},{20,28},{24,16},{28,20},{1,9},{5... | collective-permute-start | bytes 344072 | tf_op jit(solution)/shard_map/ppermute | solution.py:45
  45.1 7.2 %collective-permute-start.17 = (bf16[32,1792]{1,0:T(8,128)(2,1)S(1)}, bf16[32,1792]{1,0:T(8,128)(2,1)S(1)}, u32[]{:S(2)}, u32[]{:S(2)}) collective-permute-start(bf16[32,1792]{1,0:T(8,128)(2,1)S(1)} %get-tuple-element.66), channel_id=1, source_target_pairs={{0,12},{4,8},{8,4},{12,0},{16,28},{20,24},{24,20},{28,16},{1,13},{... | collective-permute-start | bytes 344072 | tf_op jit(solution)/shard_map/ppermute | solution.py:45
  47.0 10.6 %copy-start = (bf16[16,4,1792]{2,1,0:T(4,128)(2,1)S(1)}, bf16[16,4,1792]{2,1,0:T(4,128)(2,1)}, u32[]{:S(2)}) copy-start(bf16[16,4,1792]{2,1,0:T(4,128)(2,1)} %streams_hbm.1) | copy-start | bytes 688132
  47.7 6.9 %collective-permute-start.18 = (bf16[32,1792]{1,0:T(8,128)(2,1)S(1)}, bf16[32,1792]{1,0:T(8,128)(2,1)S(1)}, u32[]{:S(2)}, u32[]{:S(2)}) collective-permute-start(bf16[32,1792]{1,0:T(8,128)(2,1)S(1)} %get-tuple-element.61.after_ref), channel_id=1, source_target_pairs={{0,4},{4,0},{8,12},{12,8},{16,20},{20,16},{24,28},{28,24},{1,5},{5... | collective-permute-start | bytes 344072 | tf_op jit(solution)/shard_map/ppermute | solution.py:45
  54.7 6.4 %collective-permute-start.19 = (bf16[16,1792]{1,0:T(8,128)(2,1)S(1)}, bf16[16,1792]{1,0:T(8,128)(2,1)S(1)}, u32[]{:S(2)}, u32[]{:S(2)}) collective-permute-start(bf16[16,1792]{1,0:T(8,128)(2,1)S(1)} %slice.23), channel_id=1, source_target_pairs={{0,16},{4,20},{8,24},{12,28},{16,0},{20,4},{24,8},{28,12},{1,17},{... | collective-permute-start | bytes 172040 | tf_op jit(solution)/shard_map/ppermute | solution.py:45

commit v3 on v2

--- a/solution.py
+++ b/solution.py
@@ -12,7 +12,6 @@
 ITERS = 20
 EPSILON = 1e-06
 LANES = 128
-CHUNKS = 3
 
 
 F32 = jnp.float32
@@ -20,7 +19,7 @@
 IN_VMEM = pl.BlockSpec(memory_space=pltpu.VMEM)
 IN_HBM = pl.BlockSpec(memory_space=pltpu.HBM)
 IN_ANY = pl.BlockSpec(memory_space=pl.ANY)
-COPIES = 4
+COPIES = 2
 
 
 def call(body, outs, specs, aliases=None, limit=8 << 20, flops=0, scratch=()):
@@ -51,16 +50,14 @@
     while bit > 2:
         rows = jnp.concatenate((rows, flip(rows, "dp", bit)), axis=0)
         bit //= 2
-    others = [flip(rows, "dp", k) for k in range(1, 2 * bit)]
+    others = []
+    for k in range(1, 2 * bit):
+        others.append(flip(rows, "dp", k))
     return jnp.concatenate([rows] + others, axis=0), rows
 
 
-def scatter_tokens(kept, got):
-    size = lax.axis_size("dp")
-    for part in got:
-        kept = kept + part.astype(F32)
-    bit = 4
-    while bit < size:
+def scatter_tokens(kept, bit):
+    while bit < lax.axis_size("dp"):
         half = kept.shape[0] // 2
         part = flip(kept[half:].astype(BF16), "dp", bit)
         kept = kept[:half] + part.astype(F32)
@@ -81,7 +78,7 @@
     return (column // streams == row).astype(F32)
 
 
-def logits_body(streams_hbm, weight_hbm, bias_hbm, out_ref, streams_ref, bias_ref, wide_ref, weight_ref, sems):
+def logits_body(streams_hbm, weight_hbm, bias_hbm, out_ref, wide_ref, bias_ref, weight_ref, sems):
     tokens, streams, width = wide_ref.shape
     logits = weight_ref.shape[0]
     pairs = ((streams_hbm, wide_ref), (weight_hbm, weight_ref), (bias_hbm, bias_ref))
@@ -89,8 +86,6 @@
     for copy in copies:
         copy.start()
     copies[0].wait()
-    for s in range(streams):
-        streams_ref[s] = wide_ref[:, s, :]
     rows = wide_ref[...].reshape(tokens * streams, width)
     wide = rows.astype(F32)
     squares = jnp.sum(wide * wide, axis=1, keepdims=True)
@@ -112,6 +107,11 @@
     copies[2].wait()
 
 
+def turn_body(wide_ref, streams_ref):
+    for s in range(streams_ref.shape[0]):
+        streams_ref[s] = wide_ref[:, s, :]
+
+
 def mix_body(bias_ref, streams_ref, *refs):
     *part_refs, logits_ref, rows_ref = refs
     streams, tokens, width = streams_ref.shape
@@ -141,28 +141,44 @@
     out_ref[...] = jnp.concatenate([post] + rows + [spare], axis=0).T
 
 
+def copies_of(weights, outs, spans, sems):
+    copies = []
+    for weight, out, parts in zip(weights, outs, spans):
+        for first, last in parts:
+            count = 1 if (last - first) % (16 * COPIES) else COPIES
+            rows = (last - first) // count
+            for k in range(count):
+                at = pl.ds(first + k * rows, rows)
+                sem = sems.at[len(copies)]
+                copies.append(pltpu.make_async_copy(weight.at[at], out.at[at], sem))
+    return copies
+
+
+def start_now(copies):
+    @pl.when(lax.axis_index("tensor") >= 0)
+    def _():
+        for copy in copies:
+            copy.start()
+
+
 def load_body(after_ref, *refs, spans):
     n = len(spans)
-    weights, outs, sems = refs[:n], refs[-1 - n : -1], refs[-1]
-    copies = []
-    for weight, out, (first, last) in zip(weights, outs, spans):
-        count = 1 if (last - first) % (16 * COPIES) else COPIES
-        rows = (last - first) // count
-        for k in range(count):
-            at = pl.ds(first + k * rows, rows)
-            sem = sems.at[len(copies)]
-            copies.append(pltpu.make_async_copy(weight.at[at], out.at[at], sem))
+    copies = copies_of(refs[:n], refs[-1 - n : -1], spans, refs[-1])
     for copy in copies:
         copy.start()
     for copy in copies:
         copy.wait()
 
 
+def sems_for(spans):
+    return pltpu.SemaphoreType.DMA((COPIES * sum(len(parts) for parts in spans),))
+
+
 def load(after, *jobs):
-    spans = [tuple(weight.shape[0] * x // 6 for x in part) for weight, _, *part in jobs]
-    earlier = [e for _, e, *_ in jobs if e is not None]
+    spans = [parts for *_, parts in jobs]
+    earlier = [e for _, e, _ in jobs if e is not None]
     aliases, at = {}, 1 + len(jobs)
-    for k, (_, e, *_) in enumerate(jobs):
+    for k, (_, e, _) in enumerate(jobs):
         if e is not None:
             aliases[at] = k
             at += 1
@@ -173,19 +189,28 @@
         flops=int(2e9),
         limit=1 << 20,
         aliases=aliases,
-        scratch=[pltpu.SemaphoreType.DMA((COPIES * len(jobs),))],
+        scratch=[sems_for(spans)],
     )(after, *[in_hbm(weight) for weight, *_ in jobs], *earlier)
 
 
-def expand_body(after_ref, x_ref, gate_ref, up_ref, send_ref, keep_ref, *, at):
+def expand_body(after_ref, x_ref, gate_ref, up_ref, *refs, start, spans):
+    copies = []
+    if spans:
+        gate_hbm, up_hbm, send_ref, keep_ref, gate_out, up_out, sems = refs
+        copies = copies_of((gate_hbm, up_hbm), (gate_out, up_out), (spans, spans), sems)
+        start_now(copies)
+    else:
+        send_ref, keep_ref = refs
     low = lax.axis_index("tensor") % 2
     size = send_ref.shape[2]
     half = gate_ref.shape[0] // 2
     x = x_ref[...]
     for own, out in ((1 - low, send_ref), (low, keep_ref)):
-        units = pl.ds(pl.multiple_of(own * half + at * size, 8), size)
+        units = pl.ds(pl.multiple_of(own * half + start, 8), size)
         out[0] = nt(x, gate_ref[units, :]).astype(out.dtype)
         out[1] = nt(x, up_ref[units, :]).astype(out.dtype)
+    for copy in copies:
+        copy.wait()
 
 
 def part_body(keep_ref, got_ref, *refs):
@@ -231,46 +256,66 @@
         row += size
 
 
+def pool_body(kept_ref, two_ref, three_ref, *outs):
+    total = kept_ref[...] + two_ref[...].astype(F32) + three_ref[...].astype(F32)
+    row = 0
+    for out_ref in outs:
+        size = out_ref.shape[0]
+        out_ref[...] = total[row : row + size].astype(out_ref.dtype)
+        row += size
+
+
 def pieces_of(half):
-    if half % (CHUNKS * LANES):
+    if half % LANES or half < 3 * LANES:
         return [(0, half)]
-    size = half // CHUNKS
-    return [(k * size, size) for k in range(CHUNKS)]
+    tiles = half // LANES
+    last = max(1, 2 * tiles // 9)
+    middle = max(1, tiles // 3)
+    sizes = [x * LANES for x in (tiles - last - middle, middle, last)]
+    return [(sum(sizes[:k]), size) for k, size in enumerate(sizes)]
 
 
 def layer(streams, mix_weight, mix_bias, gate_weight, up_weight, down_weight):
     tokens, stream_count, width = streams.shape
     count = mix_weight.shape[0]
     shape = jax.ShapeDtypeStruct
-    partial, turned, bias = call(
+    partial, local, bias = call(
         logits_body,
         (
             shape((tokens, LANES), F32),
-            shape((stream_count, tokens, width), BF16),
+            shape(streams.shape, BF16),
             shape((1, count), F32),
         ),
         [IN_HBM] * 3,
         scratch=[
-            pltpu.VMEM(streams.shape, BF16),
             pltpu.VMEM(mix_weight.shape, BF16),
             pltpu.SemaphoreType.DMA((3,)),
         ],
     )(in_hbm(streams), in_hbm(mix_weight), in_hbm(mix_bias[None, :]))
-    parts = [partial] + [flip(partial, "tensor", k) for k in range(1, lax.axis_size("tensor"))]
-    (gate,) = load(partial, (gate_weight, None, 0, 2))
+    parts = [partial]
+    for k in range(1, lax.axis_size("tensor")):
+        parts.append(flip(partial, "tensor", k))
+    turned = call(turn_body, shape((stream_count, tokens, width), BF16), [IN_VMEM])(local)
     logits, rows = call(
         mix_body,
         (shape((tokens, LANES), F32), shape((tokens, width), BF16)),
         [IN_VMEM] * (2 + len(parts)),
     )(bias, turned, *parts)
 
-    (gate,) = load(rows, (gate_weight, gate, 2, 6))
+    half = gate_weight.shape[0] // 2
+    pieces = pieces_of(half)
+    late = pieces[-1][1] if len(pieces) > 1 else 0
+    soon = half - late
+    (gate,) = load(rows, (gate_weight, None, [(0, soon), (half, half + soon - late)]))
     rows, near_rows = gather_tokens(rows)
-    up, down = load(near_rows, (up_weight, None, 0, 6), (down_weight, None, 0, 2))
+    jobs = [(up_weight, None, [(0, soon), (half, half + soon)])]
+    if late:
+        jobs.append((gate_weight, gate, [(half + soon - late, half + soon)]))
+    up, *more = load(near_rows, *jobs)
+    gate = more[0] if late else gate
     every = rows.shape[0]
     part = every // 2
     tensor_size = lax.axis_size("tensor")
-    pieces = pieces_of(gate_weight.shape[0] // 2)
 
     def across(total, sent):
         bit = 2
@@ -283,12 +328,19 @@
     far, before = [], ()
     after = rows
     for at, (start, size) in enumerate(pieces):
-        send, keep = call(
-            functools.partial(expand_body, at=at),
-            (shape((2, every, size), BF16), shape((2, every, size), F32)),
-            [IN_ANY] + [IN_VMEM] * 3,
+        outs = [shape((2, every, size), BF16), shape((2, every, size), F32)]
+        spans = [(soon, half), (half + soon, 2 * half)] if late and not at else []
+        held = shape(gate_weight.shape, BF16)
+        send, keep, *more = call(
+            functools.partial(expand_body, start=start, spans=spans),
+            outs + ([held, held] if spans else []),
+            [IN_ANY] + [IN_VMEM] * 3 + ([IN_HBM] * 2 if spans else []),
+            aliases={2: 2, 3: 3} if spans else {},
             flops=8 * every * size * width,
-        )(after, rows, gate, up)
+            scratch=[sems_for((spans, spans))] if spans else [],
+        )(after, rows, gate, up, *([in_hbm(gate_weight), in_hbm(up_weight)] if spans else []))
+        if spans:
+            gate, up = more
         got = flip(send, "tensor", 1)
         after = send
         far_sum, far_sent, *before = call(
@@ -303,8 +355,7 @@
         )(keep, got, *before)
         far.append(across(far_sum, far_sent))
     near = [across(*before)]
-    (down,) = load(before[1], (down_weight, down, 2, 6))
-    half = gate_weight.shape[0] // 2
+    (down,) = load(before[1], (down_weight, None, [(0, 2 * half)]))
 
     def outward(pairs, after, outs):
         mine = call(
@@ -321,14 +372,25 @@
     sent = shape((step, width), BF16)
     two, three = outward(far, before[1], [sent, sent])
     got = [flip(two, "dp", 2), flip(three, "dp", 3)]
-    kept, one = outward(near, two, [shape((step, width), F32), sent])
-    got.append(flip(one, "dp", 1))
+    cut = step // 2 if lax.axis_size("dp") > 4 else step
+    kept, *ones = outward(
+        near, two, [shape((step, width), F32)] + [shape((cut, width), BF16)] * (step // cut)
+    )
+    direct = []
+    for k, one in enumerate(ones):
+        direct.append(flip(one, "dp", 1 + 4 * k))
+    mlp_out, *rest = call(
+        pool_body,
+        [shape((cut, width), F32)] + [shape((cut, width), BF16)] * (step // cut - 1),
+        [IN_VMEM] * (1 + len(got)),
+    )(kept, *got)
+    direct += [flip(part_sum, "dp", 4) for part_sum in rest]
     mixing = call(
         functools.partial(sinkhorn_body, streams=stream_count),
         shape((tokens, LANES), F32),
         [IN_ANY, IN_VMEM],
         flops=int(1e9),
-    )(one, logits)
+    )((rest or ones)[0], logits)
     post_gate = mixing[:, :stream_count]
     entries = mixing[:, stream_count : stream_count + stream_count**2]
     res_mix = entries.reshape(tokens, stream_count, stream_count)
@@ -336,7 +398,9 @@
         "tij,tjc->tic", res_mix, streams.astype(F32), precision=lax.Precision.HIGHEST
     )
     mixed, post_gate = lax.optimization_barrier((mixed, post_gate))
-    mlp_out = scatter_tokens(kept, got)
+    for part_sum in direct:
+        mlp_out = mlp_out + part_sum.astype(F32)
+    mlp_out = scatter_tokens(mlp_out, 8)
     mixed = mixed + post_gate[:, :, None] * mlp_out[:, None, :]
     return mixed.astype(BF16)
 

time: 62.1 us -> 63.8 us (1.027)
  waiting for transfers between devices: 16.2 us -> 19 us
  Pallas kernels: 22.2 us -> 20.9 us
    ppermute x20 -> x21, waiting for transfers between devices: 16.2 us -> 19 us  [flip(): return lax.ppermute(value, axis, [(i, i ^ bits) for i in range(size)])]
    pallas_call x4 -> x3, Pallas kernels: 11.2 us -> 9.17 us  [load(): call(functools.partial(load_body, spans=spans), tuple((jax.ShapeDtypeStru...]
    pallas_call x4 -> x6, Pallas kernels: 6.96 us -> 7.69 us  [the longest x3 5.51 us: layer(): call(functools.partial(expand_body, start=start, spans=spans), outs + ([h...]
    ppermute x20 -> x21, starting transfers between devices: 21.6 us -> 21.8 us  [flip(): return lax.ppermute(value, axis, [(i, i ^ bits) for i in range(size)])]
  transfers between devices with their start and end apart: 20 -> 21, of which waited for: 9 -> 9; matrix products, arithmetic and copies ran while one was open for 1% -> 1% of each run, Pallas kernels for 29% -> 26%
where the time goes in v3:
time: 63.8 us; the launch traced here: 63.6 us
  starting transfers between devices  21.8 us (34%)
  Pallas kernels  20.9 us (33%)
  waiting for transfers between devices  19 us (30%)
  other arithmetic  0.9 us (1%)
    ppermute x21, starting transfers between devices, flip(): return lax.ppermute(value, axis, [(i, i ^ bits) for i in range(size)])  21.8 us
    ppermute x21, waiting for transfers between devices, flip(): return lax.ppermute(value, axis, [(i, i ^ bits) for i in range(size)])  19 us
    pallas_call x3, Pallas kernels, load(): call(functools.partial(load_body, spans=spans), tuple((jax.ShapeDtypeStru...  9.17 us
    pallas_call x3, Pallas kernels, layer(): call(functools.partial(expand_body, start=start, spans=spans), outs + ([h...  5.51 us
    pallas_call x1, Pallas kernels, layer(): call(logits_body, (shape((tokens, LANES), F32), shape(streams.shape, BF16...  1.71 us
    pallas_call x2, Pallas kernels, outward(): return call(other_body, outs, [IN_VMEM] * 3, flops=flops)(own, other, down)  1.42 us
    pallas_call x2, Pallas kernels, outward(): call(own_body, shape((part, width), F32), [IN_VMEM] * 2, flops=flops)  1.39 us
  transfers between devices with their start and end apart: 21, of which 9 were waited for; matrix products, arithmetic and copies ran while one was open for 1% of the time, Pallas kernels for 26%

profile of v3, /device:TPU:0, one launch (start us, length us, event | category | flops | bytes accessed | tf_op | source)
XLA Modules:
  0.0 63.6 jit_solution(10424157265398853428)
XLA Ops:
  0.0 1.7 %shard_map.64 = (f32[16,128]{1,0:T(8,128)S(1)}, bf16[16,4,1792]{2,1,0:T(4,128)(2,1)S(1)}, f32[1,24]{1,0:T(1,128)S(1)}) custom-call(bf16[16,4,1792]{2,1,0:T(4,128)(2,1)} %streams_hbm.1, bf16[24,4,1792]{2,1,0:T(4,128)(2,1)} %weight_hbm.1, f32[1,24]{1,0:T(1,128)} %bitcast.7), custom_call_target="tpu_custom_call" | custom-call | tf_op jit(solution)/shard_map/pallas_call | solution.py:282
  1.7 2.5 %collective-permute-start.2 = (f32[16,128]{1,0:T(8,128)S(1)}, f32[16,128]{1,0:T(8,128)S(1)}, u32[]{:S(2)}, u32[]{:S(2)}) collective-permute-start(f32[16,128]{1,0:T(8,128)S(1)} %get-tuple-element.43.refs_0_), channel_id=1, source_target_pairs={{0,3},{1,2},{2,1},{3,0},{4,7},{5,6},{6,5},{7,4},{8,11},{9,10},{10,... | collective-permute-start | bytes 24584 | tf_op jit(solution)/shard_map/ppermute | solution.py:44
  5.6 2.3 %collective-permute-done.1.refs_2_ = f32[16,128]{1,0:T(8,128)S(1)} collective-permute-done((f32[16,128]{1,0:T(8,128)S(1)}, f32[16,128]{1,0:T(8,128)S(1)}, u32[]{:S(2)}, u32[]{:S(2)}) %collective-permute-start.1) | collective-permute-done | bytes 8224 | tf_op jit(solution)/shard_map/ppermute | solution.py:44
  8.1 2.7 %collective-permute-start.3 = (bf16[16,1792]{1,0:T(8,128)(2,1)S(1)}, bf16[16,1792]{1,0:T(8,128)(2,1)S(1)}, u32[]{:S(2)}, u32[]{:S(2)}) collective-permute-start(bf16[16,1792]{1,0:T(8,128)(2,1)S(1)} %get-tuple-element.44.after_ref), channel_id=1, source_target_pairs={{0,16},{4,20},{8,24},{12,28},{16,0},{20,4},{24,8},{28,12},{1,17},{... | collective-permute-start | bytes 172040 | tf_op jit(solution)/shard_map/ppermute | solution.py:44
  10.7 2.6 %shard_map.67.refs_2_ = bf16[2304,1792]{1,0:T(8,128)(2,1)S(1)} custom-call(bf16[16,1792]{1,0:T(8,128)(2,1)S(1)} %get-tuple-element.44.after_ref, bf16[2304,1792]{1,0:T(8,128)(2,1)} %refs_0_.6), custom_call_target="tpu_custom_call" | custom-call | flops 2000000000 | tf_op jit(solution)/shard_map/pallas_call | solution.py:185
  13.4 2.5 %collective-permute-start.6 = (bf16[32,1792]{1,0:T(8,128)(2,1)S(1)}, bf16[32,1792]{1,0:T(8,128)(2,1)S(1)}, u32[]{:S(2)}, u32[]{:S(2)}) collective-permute-start(bf16[32,1792]{1,0:T(8,128)(2,1)S(1)} %get-tuple-element.77.after_ref), channel_id=1, source_target_pairs={{0,12},{4,8},{8,4},{12,0},{16,28},{20,24},{24,20},{28,16},{1,13},{... | collective-permute-start | bytes 344072 | tf_op jit(solution)/shard_map/ppermute | solution.py:44
  17.0 3.1 %shard_map.68 = (bf16[2304,1792]{1,0:T(8,128)(2,1)S(1)}, bf16[2304,1792]{1,0:T(8,128)(2,1)S(1)}) custom-call(bf16[32,1792]{1,0:T(8,128)(2,1)S(1)} %get-tuple-element.77.after_ref, bf16[2304,1792]{1,0:T(8,128)(2,1)} %refs_1_.3, bf16[2304,1792]{1,0:T(8,128)(2,1)} %refs_0_.6, bf16[2304,1792]{1,0:T(8,128)(2,1)S(1)} %shard_map.67.refs_2_), custom_call_target="tpu_custom_call", output_to_operand_aliasing={{1}: (3, {})} | custom-call | flops 2000000000 | tf_op jit(solution)/shard_map/pallas_call | solution.py:185
  20.1 1.3 %collective-permute-done.4 = bf16[32,1792]{1,0:T(8,128)(2,1)S(1)} collective-permute-done((bf16[32,1792]{1,0:T(8,128)(2,1)S(1)}, bf16[32,1792]{1,0:T(8,128)(2,1)S(1)}, u32[]{:S(2)}, u32[]{:S(2)}) %collective-permute-start.4) | collective-permute-done | bytes 114720 | tf_op jit(solution)/shard_map/ppermute | solution.py:44
  21.5 2.6 %shard_map.69 = (bf16[2,128,512]{2,1,0:T(8,128)(2,1)S(1)}, f32[2,128,512]{2,1,0:T(8,128)S(1)}, bf16[2304,1792]{1,0:T(8,128)(2,1)S(1)}, bf16[2304,1792]{1,0:T(8,128)(2,1)S(1)}) custom-call(bf16[128,1792]{1,0:T(8,128)(2,1)S(1)} %constant_dynamic-update-slice_fusion.2.after_ref.x_ref, ...), custom_call_target="tpu_custom_call", output_to_operand_aliasing={{2}: (2, {}), {3}: (3, {})} | custom-call | flops 939524096 | tf_op jit(solution)/shard_map/pallas_call | solution.py:334
  24.1 1.6 %shard_map.70 = (bf16[2,128,384]{2,1,0:T(8,128)(2,1)S(1)}, f32[2,128,384]{2,1,0:T(8,128)S(1)}) custom-call(bf16[2,128,512]{2,1,0:T(8,128)(2,1)S(1)} %get-tuple-element.47.after_ref, bf16[128,1792]{1,0:T(8,128)(2,1)S(1)} %constant_dynamic-update-slice_fusion.2.after_ref.x_ref, bf16[2304,1792]{1,0:T(8,128)(2,1)S(1)} %get-tuple-element.48.gate_ref, ...), custom_call_target="tpu_custom_call" | custom-call | flops 704643072 | tf_op jit(solution)/shard_map/pallas_call | solution.py:334
  26.3 1.3 %shard_map.71 = (bf16[2,128,256]{2,1,0:T(8,128)(2,1)S(1)}, f32[2,128,256]{2,1,0:T(8,128)S(1)}) custom-call(bf16[2,128,384]{2,1,0:T(8,128)(2,1)S(1)} %get-tuple-element.50.after_ref, bf16[128,1792]{1,0:T(8,128)(2,1)S(1)} %constant_dynamic-update-slice_fusion.2.after_ref.x_ref, bf16[2304,1792]{1,0:T(8,128)(2,1)S(1)} %get-tuple-element.48.gate_ref, ...), custom_call_target="tpu_custom_call" | custom-call | flops 469762048 | tf_op jit(solution)/shard_map/pallas_call | solution.py:334
  27.8 0.7 %collective-permute-start.10 = (bf16[2,64,512]{2,1,0:T(8,128)(2,1)S(1)}, bf16[2,64,512]{2,1,0:T(8,128)(2,1)S(1)}, u32[]{:S(2)}, u32[]{:S(2)}) collective-permute-start(bf16[2,64,512]{2,1,0:T(8,128)(2,1)S(1)} %get-tuple-element.61), channel_id=1, source_target_pairs={{0,2},{1,3},{2,0},{3,1},{4,6},{5,7},{6,4},{7,5},{8,10},{9,11},{10,... | collective-permute-start | bytes 393224 | tf_op jit(solution)/shard_map/ppermute | solution.py:44
  28.6 1.5 %collective-permute-start.11 = (bf16[2,64,384]{2,1,0:T(8,128)(2,1)S(1)}, bf16[2,64,384]{2,1,0:T(8,128)(2,1)S(1)}, u32[]{:S(2)}, u32[]{:S(2)}) collective-permute-start(bf16[2,64,384]{2,1,0:T(8,128)(2,1)S(1)} %get-tuple-element.63), channel_id=1, source_target_pairs={{0,2},{1,3},{2,0},{3,1},{4,6},{5,7},{6,4},{7,5},{8,10},{9,11},{10,... | collective-permute-start | bytes 294920 | tf_op jit(solution)/shard_map/ppermute | solution.py:44
  30.1 0.7 %collective-permute-start.12 = (bf16[2,64,256]{2,1,0:T(8,128)(2,1)S(1)}, bf16[2,64,256]{2,1,0:T(8,128)(2,1)S(1)}, u32[]{:S(2)}, u32[]{:S(2)}) collective-permute-start(bf16[2,64,256]{2,1,0:T(8,128)(2,1)S(1)} %get-tuple-element.65), channel_id=1, source_target_pairs={{0,2},{1,3},{2,0},{3,1},{4,6},{5,7},{6,4},{7,5},{8,10},{9,11},{10,... | collective-permute-start | bytes 196616 | tf_op jit(solution)/shard_map/ppermute | solution.py:44
  30.8 1.4 %collective-permute-start.14 = (bf16[2,64,1152]{2,1,0:T(8,128)(2,1)S(1)}, bf16[2,64,1152]{2,1,0:T(8,128)(2,1)S(1)}, u32[]{:S(2)}, u32[]{:S(2)}) collective-permute-start(bf16[2,64,1152]{2,1,0:T(8,128)(2,1)S(1)} %get-tuple-element.59.after_ref), channel_id=1, source_target_pairs={{0,2},{1,3},{2,0},{3,1},{4,6},{5,7},{6,4},{7,5},{8,10},{9,11},{10,... | collective-permute-start | bytes 884744 | tf_op jit(solution)/shard_map/ppermute | solution.py:44
  32.2 5.5 %collective-permute-done.12.refs_5_ = bf16[2,64,256]{2,1,0:T(8,128)(2,1)S(1)} collective-permute-done((bf16[2,64,256]{2,1,0:T(8,128)(2,1)S(1)}, bf16[2,64,256]{2,1,0:T(8,128)(2,1)S(1)}, u32[]{:S(2)}, u32[]{:S(2)}) %collective-permute-start.12) | collective-permute-done | bytes 65568 | tf_op jit(solution)/shard_map/ppermute | solution.py:44
  37.9 3.4 %shard_map.76.down_ref = bf16[2304,1792]{1,0:T(8,128)(2,1)S(1)} custom-call(bf16[2,64,1152]{2,1,0:T(8,128)(2,1)S(1)} %get-tuple-element.59.after_ref, bf16[2304,1792]{1,0:T(8,128)(2,1)} %refs_0_.7), custom_call_target="tpu_custom_call" | custom-call | flops 2000000000 | tf_op jit(solution)/shard_map/pallas_call | solution.py:185
  41.4 0.7 %shard_map.77.own_ref = f32[64,1792]{1,0:T(8,128)S(1)} custom-call(bf16[64,1152]{1,0:T(8,128)(2,1)S(1)} %shard_map.75.mine_ref, bf16[2304,1792]{1,0:T(8,128)(2,1)S(1)} %shard_map.76.down_ref), custom_call_target="tpu_custom_call" | custom-call | flops 264241152 | tf_op jit(solution)/shard_map/pallas_call | solution.py:368
  42.1 0.7 %shard_map.78 = (bf16[32,1792]{1,0:T(8,128)(2,1)S(1)}, bf16[32,1792]{1,0:T(8,128)(2,1)S(1)}) custom-call(f32[64,1792]{1,0:T(8,128)S(1)} %shard_map.77.own_ref, bf16[64,1152]{1,0:T(8,128)(2,1)S(1)} %collective-permute-done.13.other_ref, bf16[2304,1792]{1,0:T(8,128)(2,1)S(1)} %shard_map.76.down_ref), custom_call_target="tpu_custom_call" | custom-call | flops 264241152 | tf_op jit(solution)/shard_map/pallas_call | solution.py:369
  42.8 0.8 %collective-permute-done.14.refs_1_ = bf16[2,64,1152]{2,1,0:T(8,128)(2,1)S(1)} collective-permute-done((bf16[2,64,1152]{2,1,0:T(8,128)(2,1)S(1)}, bf16[2,64,1152]{2,1,0:T(8,128)(2,1)S(1)}, u32[]{:S(2)}, u32[]{:S(2)}) %collective-permute-start.14) | collective-permute-done | bytes 294944 | tf_op jit(solution)/shard_map/ppermute | solution.py:44
  43.7 2.3 %collective-permute-start.17 = (bf16[32,1792]{1,0:T(8,128)(2,1)S(1)}, bf16[32,1792]{1,0:T(8,128)(2,1)S(1)}, u32[]{:S(2)}, u32[]{:S(2)}) collective-permute-start(bf16[32,1792]{1,0:T(8,128)(2,1)S(1)} %get-tuple-element.69), channel_id=1, source_target_pairs={{0,12},{4,8},{8,4},{12,0},{16,28},{20,24},{24,20},{28,16},{1,13},{... | collective-permute-start | bytes 344072 | tf_op jit(solution)/shard_map/ppermute | solution.py:44
  46.5 0.7 %shard_map.80.own_ref = f32[64,1792]{1,0:T(8,128)S(1)} custom-call(bf16[64,1152]{1,0:T(8,128)(2,1)S(1)} %shard_map.79.mine_ref, bf16[2304,1792]{1,0:T(8,128)(2,1)S(1)} %shard_map.76.down_ref), custom_call_target="tpu_custom_call" | custom-call | flops 264241152 | tf_op jit(solution)/shard_map/pallas_call | solution.py:368
  47.2 0.7 %shard_map.81 = (f32[32,1792]{1,0:T(8,128)S(1)}, bf16[16,1792]{1,0:T(8,128)(2,1)S(1)}, bf16[16,1792]{1,0:T(8,128)(2,1)S(1)}) custom-call(f32[64,1792]{1,0:T(8,128)S(1)} %shard_map.80.own_ref, bf16[64,1152]{1,0:T(8,128)(2,1)S(1)} %collective-permute-done.15.other_ref, bf16[2304,1792]{1,0:T(8,128)(2,1)S(1)} %shard_map.76.down_ref), custom_call_target="tpu_custom_call" | custom-call | flops 264241152 | tf_op jit(solution)/shard_map/pallas_call | solution.py:369
  47.9 2.8 %collective-permute-done.17.three_ref = bf16[32,1792]{1,0:T(8,128)(2,1)S(1)} collective-permute-done((bf16[32,1792]{1,0:T(8,128)(2,1)S(1)}, bf16[32,1792]{1,0:T(8,128)(2,1)S(1)}, u32[]{:S(2)}, u32[]{:S(2)}) %collective-permute-start.17) | collective-permute-done | bytes 114720 | tf_op jit(solution)/shard_map/ppermute | solution.py:44
  50.7 1.7 %collective-permute-done.16.two_ref = bf16[32,1792]{1,0:T(8,128)(2,1)S(1)} collective-permute-done((bf16[32,1792]{1,0:T(8,128)(2,1)S(1)}, bf16[32,1792]{1,0:T(8,128)(2,1)S(1)}, u32[]{:S(2)}, u32[]{:S(2)}) %collective-permute-start.16) | collective-permute-done | bytes 114720 | tf_op jit(solution)/shard_map/ppermute | solution.py:44
  52.4 2.2 %collective-permute-start.20 = (bf16[16,1792]{1,0:T(8,128)(2,1)S(1)}, bf16[16,1792]{1,0:T(8,128)(2,1)S(1)}, u32[]{:S(2)}, u32[]{:S(2)}) collective-permute-start(bf16[16,1792]{1,0:T(8,128)(2,1)S(1)} %get-tuple-element.70.after_ref), channel_id=1, source_target_pairs={{0,16},{4,20},{8,24},{12,28},{16,0},{20,4},{24,8},{28,12},{1,17},{... | collective-permute-start | bytes 172040 | tf_op jit(solution)/shard_map/ppermute | solution.py:44
  54.6 0.7 %shard_map.83 = f32[16,128]{1,0:T(8,128)S(1)} custom-call(bf16[16,1792]{1,0:T(8,128)(2,1)S(1)} %get-tuple-element.70.after_ref, f32[16,128]{1,0:T(8,128)S(1)} %get-tuple-element.71.logits_ref), custom_call_target="tpu_custom_call" | custom-call | flops 1000000000 | tf_op jit(solution)/shard_map/pallas_call | solution.py:388
  55.6 1.0 %collective-permute-start.18 = (bf16[16,1792]{1,0:T(8,128)(2,1)S(1)}, bf16[16,1792]{1,0:T(8,128)(2,1)S(1)}, u32[]{:S(2)}, u32[]{:S(2)}) collective-permute-start(bf16[16,1792]{1,0:T(8,128)(2,1)S(1)} %get-tuple-element.75), channel_id=1, source_target_pairs={{0,4},{4,0},{8,12},{12,8},{16,20},{20,16},{24,28},{28,24},{1,5},{5... | collective-permute-start | bytes 172040 | tf_op jit(solution)/shard_map/ppermute | solution.py:44
  56.6 1.3 %collective-permute-start.19 = (bf16[16,1792]{1,0:T(8,128)(2,1)S(1)}, bf16[16,1792]{1,0:T(8,128)(2,1)S(1)}, u32[]{:S(2)}, u32[]{:S(2)}) collective-permute-start(bf16[16,1792]{1,0:T(8,128)(2,1)S(1)} %get-tuple-element.76), channel_id=1, source_target_pairs={{0,20},{4,16},{8,28},{12,24},{16,4},{20,0},{24,12},{28,8},{1,21},{... | collective-permute-start | bytes 172040 | tf_op jit(solution)/shard_map/ppermute | solution.py:44
  58.4 1.4 %collective-permute-done.18 = bf16[16,1792]{1,0:T(8,128)(2,1)S(1)} collective-permute-done((bf16[16,1792]{1,0:T(8,128)(2,1)S(1)}, bf16[16,1792]{1,0:T(8,128)(2,1)S(1)}, u32[]{:S(2)}, u32[]{:S(2)}) %collective-permute-start.18) | collective-permute-done | bytes 57376 | tf_op jit(solution)/shard_map/ppermute | solution.py:44
  59.8 2.9 %collective-permute-done.19 = bf16[16,1792]{1,0:T(8,128)(2,1)S(1)} collective-permute-done((bf16[16,1792]{1,0:T(8,128)(2,1)S(1)}, bf16[16,1792]{1,0:T(8,128)(2,1)S(1)}, u32[]{:S(2)}, u32[]{:S(2)}) %collective-permute-start.19) | collective-permute-done | bytes 57376 | tf_op jit(solution)/shard_map/ppermute | solution.py:44
  62.8 0.9 %add_convert_fusion = bf16[16,4,1792]{2,1,0:T(4,128)(2,1)} fusion(f32[16,4,1792]{2,1,0:T(4,128)S(1)} %fusion, f32[16,1792]{1,0:T(8,128)S(1)} %convert_add_fusion, f32[16,4]{1,0:T(8,128)S(1)} %bitcast.5), kind=kLoop, calls=%fused_computation | loop fusion | flops 344064 | bytes 803072 | tf_op jit(solution)/shard_map/convert_element_type | solution.py:405
  (43 shorter events, 5.3 us)
Async XLA Ops:
  1.7 3.9 %collective-permute-start.2 = (f32[16,128]{1,0:T(8,128)S(1)}, f32[16,128]{1,0:T(8,128)S(1)}, u32[]{:S(2)}, u32[]{:S(2)}) collective-permute-start(f32[16,128]{1,0:T(8,128)S(1)} %get-tuple-element.43.refs_0_), channel_id=1, source_target_pairs={{0,3},{1,2},{2,1},{3,0},{4,7},{5,6},{6,5},{7,4},{8,11},{9,10},{10,... | collective-permute-start | bytes 24584 | tf_op jit(solution)/shard_map/ppermute | solution.py:44
  4.2 3.7 %collective-permute-start.1 = (f32[16,128]{1,0:T(8,128)S(1)}, f32[16,128]{1,0:T(8,128)S(1)}, u32[]{:S(2)}, u32[]{:S(2)}) collective-permute-start(f32[16,128]{1,0:T(8,128)S(1)} %get-tuple-element.43.refs_0_), channel_id=1, source_target_pairs={{0,2},{1,3},{2,0},{3,1},{4,6},{5,7},{6,4},{7,5},{8,10},{9,11},{10,... | collective-permute-start | bytes 24584 | tf_op jit(solution)/shard_map/ppermute | solution.py:44
  4.9 3.0 %collective-permute-start = (f32[16,128]{1,0:T(8,128)S(1)}, f32[16,128]{1,0:T(8,128)S(1)}, u32[]{:S(2)}, u32[]{:S(2)}) collective-permute-start(f32[16,128]{1,0:T(8,128)S(1)} %get-tuple-element.43.refs_0_), channel_id=1, source_target_pairs={{0,1},{1,0},{2,3},{3,2},{4,5},{5,4},{6,7},{7,6},{8,9},{9,8},{10,11... | collective-permute-start | bytes 24584 | tf_op jit(solution)/shard_map/ppermute | solution.py:44
  8.1 5.3 %collective-permute-start.3 = (bf16[16,1792]{1,0:T(8,128)(2,1)S(1)}, bf16[16,1792]{1,0:T(8,128)(2,1)S(1)}, u32[]{:S(2)}, u32[]{:S(2)}) collective-permute-start(bf16[16,1792]{1,0:T(8,128)(2,1)S(1)} %get-tuple-element.44.after_ref), channel_id=1, source_target_pairs={{0,16},{4,20},{8,24},{12,28},{16,0},{20,4},{24,8},{28,12},{1,17},{... | collective-permute-start | bytes 172040 | tf_op jit(solution)/shard_map/ppermute | solution.py:44
  13.4 8.0 %collective-permute-start.6 = (bf16[32,1792]{1,0:T(8,128)(2,1)S(1)}, bf16[32,1792]{1,0:T(8,128)(2,1)S(1)}, u32[]{:S(2)}, u32[]{:S(2)}) collective-permute-start(bf16[32,1792]{1,0:T(8,128)(2,1)S(1)} %get-tuple-element.77.after_ref), channel_id=1, source_target_pairs={{0,12},{4,8},{8,4},{12,0},{16,28},{20,24},{24,20},{28,16},{1,13},{... | collective-permute-start | bytes 344072 | tf_op jit(solution)/shard_map/ppermute | solution.py:44
  16.0 5.4 %collective-permute-start.5 = (bf16[32,1792]{1,0:T(8,128)(2,1)S(1)}, bf16[32,1792]{1,0:T(8,128)(2,1)S(1)}, u32[]{:S(2)}, u32[]{:S(2)}) collective-permute-start(bf16[32,1792]{1,0:T(8,128)(2,1)S(1)} %get-tuple-element.77.after_ref), channel_id=1, source_target_pairs={{0,8},{4,12},{8,0},{12,4},{16,24},{20,28},{24,16},{28,20},{1,9},{5... | collective-permute-start | bytes 344072 | tf_op jit(solution)/shard_map/ppermute | solution.py:44
  16.4 4.9 %collective-permute-start.4 = (bf16[32,1792]{1,0:T(8,128)(2,1)S(1)}, bf16[32,1792]{1,0:T(8,128)(2,1)S(1)}, u32[]{:S(2)}, u32[]{:S(2)}) collective-permute-start(bf16[32,1792]{1,0:T(8,128)(2,1)S(1)} %get-tuple-element.77.after_ref), channel_id=1, source_target_pairs={{0,4},{4,0},{8,12},{12,8},{16,20},{20,16},{24,28},{28,24},{1,5},{5... | collective-permute-start | bytes 344072 | tf_op jit(solution)/shard_map/ppermute | solution.py:44
  24.0 3.7 %collective-permute-start.9 = (bf16[2,128,512]{2,1,0:T(8,128)(2,1)S(1)}, bf16[2,128,512]{2,1,0:T(8,128)(2,1)S(1)}, u32[]{:S(2)}, u32[]{:S(2)}) collective-permute-start(bf16[2,128,512]{2,1,0:T(8,128)(2,1)S(1)} %get-tuple-element.47.after_ref), channel_id=1, source_target_pairs={{0,1},{1,0},{2,3},{3,2},{4,5},{5,4},{6,7},{7,6},{8,9},{9,8},{10,11... | collective-permute-start | bytes 786440 | tf_op jit(solution)/shard_map/ppermute | solution.py:44
  25.8 2.7 %collective-permute-start.8 = (bf16[2,128,384]{2,1,0:T(8,128)(2,1)S(1)}, bf16[2,128,384]{2,1,0:T(8,128)(2,1)S(1)}, u32[]{:S(2)}, u32[]{:S(2)}) collective-permute-start(bf16[2,128,384]{2,1,0:T(8,128)(2,1)S(1)} %get-tuple-element.50.after_ref), channel_id=1, source_target_pairs={{0,1},{1,0},{2,3},{3,2},{4,5},{5,4},{6,7},{7,6},{8,9},{9,8},{10,11... | collective-permute-start | bytes 589832 | tf_op jit(solution)/shard_map/ppermute | solution.py:44
  27.6 2.4 %collective-permute-start.7 = (bf16[2,128,256]{2,1,0:T(8,128)(2,1)S(1)}, bf16[2,128,256]{2,1,0:T(8,128)(2,1)S(1)}, u32[]{:S(2)}, u32[]{:S(2)}) collective-permute-start(bf16[2,128,256]{2,1,0:T(8,128)(2,1)S(1)} %get-tuple-element.52), channel_id=1, source_target_pairs={{0,1},{1,0},{2,3},{3,2},{4,5},{5,4},{6,7},{7,6},{8,9},{9,8},{10,11... | collective-permute-start | bytes 393224 | tf_op jit(solution)/shard_map/ppermute | solution.py:44
  27.8 10.0 %collective-permute-start.10 = (bf16[2,64,512]{2,1,0:T(8,128)(2,1)S(1)}, bf16[2,64,512]{2,1,0:T(8,128)(2,1)S(1)}, u32[]{:S(2)}, u32[]{:S(2)}) collective-permute-start(bf16[2,64,512]{2,1,0:T(8,128)(2,1)S(1)} %get-tuple-element.61), channel_id=1, source_target_pairs={{0,2},{1,3},{2,0},{3,1},{4,6},{5,7},{6,4},{7,5},{8,10},{9,11},{10,... | collective-permute-start | bytes 393224 | tf_op jit(solution)/shard_map/ppermute | solution.py:44
  28.6 9.2 %collective-permute-start.11 = (bf16[2,64,384]{2,1,0:T(8,128)(2,1)S(1)}, bf16[2,64,384]{2,1,0:T(8,128)(2,1)S(1)}, u32[]{:S(2)}, u32[]{:S(2)}) collective-permute-start(bf16[2,64,384]{2,1,0:T(8,128)(2,1)S(1)} %get-tuple-element.63), channel_id=1, source_target_pairs={{0,2},{1,3},{2,0},{3,1},{4,6},{5,7},{6,4},{7,5},{8,10},{9,11},{10,... | collective-permute-start | bytes 294920 | tf_op jit(solution)/shard_map/ppermute | solution.py:44
  30.1 7.6 %collective-permute-start.12 = (bf16[2,64,256]{2,1,0:T(8,128)(2,1)S(1)}, bf16[2,64,256]{2,1,0:T(8,128)(2,1)S(1)}, u32[]{:S(2)}, u32[]{:S(2)}) collective-permute-start(bf16[2,64,256]{2,1,0:T(8,128)(2,1)S(1)} %get-tuple-element.65), channel_id=1, source_target_pairs={{0,2},{1,3},{2,0},{3,1},{4,6},{5,7},{6,4},{7,5},{8,10},{9,11},{10,... | collective-permute-start | bytes 196616 | tf_op jit(solution)/shard_map/ppermute | solution.py:44
  30.8 12.8 %collective-permute-start.14 = (bf16[2,64,1152]{2,1,0:T(8,128)(2,1)S(1)}, bf16[2,64,1152]{2,1,0:T(8,128)(2,1)S(1)}, u32[]{:S(2)}, u32[]{:S(2)}) collective-permute-start(bf16[2,64,1152]{2,1,0:T(8,128)(2,1)S(1)} %get-tuple-element.59.after_ref), channel_id=1, source_target_pairs={{0,2},{1,3},{2,0},{3,1},{4,6},{5,7},{6,4},{7,5},{8,10},{9,11},{10,... | collective-permute-start | bytes 884744 | tf_op jit(solution)/shard_map/ppermute | solution.py:44
  37.8 4.2 %collective-permute-start.13 = (bf16[64,1152]{1,0:T(8,128)(2,1)S(1)}, bf16[64,1152]{1,0:T(8,128)(2,1)S(1)}, u32[]{:S(2)}, u32[]{:S(2)}) collective-permute-start(bf16[64,1152]{1,0:T(8,128)(2,1)S(1)} %shard_map.75.mine_ref), channel_id=1, source_target_pairs={{0,1},{1,0},{2,3},{3,2},{4,5},{5,4},{6,7},{7,6},{8,9},{9,8},{10,11... | collective-permute-start | bytes 442376 | tf_op jit(solution)/shard_map/ppermute | solution.py:44
  43.6 3.5 %collective-permute-start.15 = (bf16[64,1152]{1,0:T(8,128)(2,1)S(1)}, bf16[64,1152]{1,0:T(8,128)(2,1)S(1)}, u32[]{:S(2)}, u32[]{:S(2)}) collective-permute-start(bf16[64,1152]{1,0:T(8,128)(2,1)S(1)} %shard_map.79.mine_ref), channel_id=1, source_target_pairs={{0,1},{1,0},{2,3},{3,2},{4,5},{5,4},{6,7},{7,6},{8,9},{9,8},{10,11... | collective-permute-start | bytes 442376 | tf_op jit(solution)/shard_map/ppermute | solution.py:44
  43.7 7.0 %collective-permute-start.17 = (bf16[32,1792]{1,0:T(8,128)(2,1)S(1)}, bf16[32,1792]{1,0:T(8,128)(2,1)S(1)}, u32[]{:S(2)}, u32[]{:S(2)}) collective-permute-start(bf16[32,1792]{1,0:T(8,128)(2,1)S(1)} %get-tuple-element.69), channel_id=1, source_target_pairs={{0,12},{4,8},{8,4},{12,0},{16,28},{20,24},{24,20},{28,16},{1,13},{... | collective-permute-start | bytes 344072 | tf_op jit(solution)/shard_map/ppermute | solution.py:44
  46.0 6.4 %collective-permute-start.16 = (bf16[32,1792]{1,0:T(8,128)(2,1)S(1)}, bf16[32,1792]{1,0:T(8,128)(2,1)S(1)}, u32[]{:S(2)}, u32[]{:S(2)}) collective-permute-start(bf16[32,1792]{1,0:T(8,128)(2,1)S(1)} %get-tuple-element.66.after_ref), channel_id=1, source_target_pairs={{0,8},{4,12},{8,0},{12,4},{16,24},{20,28},{24,16},{28,20},{1,9},{5... | collective-permute-start | bytes 344072 | tf_op jit(solution)/shard_map/ppermute | solution.py:44
  47.2 10.7 %copy-start = (bf16[16,4,1792]{2,1,0:T(4,128)(2,1)S(1)}, bf16[16,4,1792]{2,1,0:T(4,128)(2,1)}, u32[]{:S(2)}) copy-start(bf16[16,4,1792]{2,1,0:T(4,128)(2,1)} %streams_hbm.1) | copy-start | bytes 688132
  52.4 6.0 %collective-permute-start.20 = (bf16[16,1792]{1,0:T(8,128)(2,1)S(1)}, bf16[16,1792]{1,0:T(8,128)(2,1)S(1)}, u32[]{:S(2)}, u32[]{:S(2)}) collective-permute-start(bf16[16,1792]{1,0:T(8,128)(2,1)S(1)} %get-tuple-element.70.after_ref), channel_id=1, source_target_pairs={{0,16},{4,20},{8,24},{12,28},{16,0},{20,4},{24,8},{28,12},{1,17},{... | collective-permute-start | bytes 172040 | tf_op jit(solution)/shard_map/ppermute | solution.py:44
  55.6 4.2 %collective-permute-start.18 = (bf16[16,1792]{1,0:T(8,128)(2,1)S(1)}, bf16[16,1792]{1,0:T(8,128)(2,1)S(1)}, u32[]{:S(2)}, u32[]{:S(2)}) collective-permute-start(bf16[16,1792]{1,0:T(8,128)(2,1)S(1)} %get-tuple-element.75), channel_id=1, source_target_pairs={{0,4},{4,0},{8,12},{12,8},{16,20},{20,16},{24,28},{28,24},{1,5},{5... | collective-permute-start | bytes 172040 | tf_op jit(solution)/shard_map/ppermute | solution.py:44
  56.6 6.1 %collective-permute-start.19 = (bf16[16,1792]{1,0:T(8,128)(2,1)S(1)}, bf16[16,1792]{1,0:T(8,128)(2,1)S(1)}, u32[]{:S(2)}, u32[]{:S(2)}) collective-permute-start(bf16[16,1792]{1,0:T(8,128)(2,1)S(1)} %get-tuple-element.76), channel_id=1, source_target_pairs={{0,20},{4,16},{8,28},{12,24},{16,4},{20,0},{24,12},{28,8},{1,21},{... | collective-permute-start | bytes 172040 | tf_op jit(solution)/shard_map/ppermute | solution.py:44

commit v4 on v3

--- a/solution.py
+++ b/solution.py
@@ -94,12 +94,8 @@
     token = lax.broadcasted_iota(jnp.int32, pairs.shape, 0)
     logit = lax.broadcasted_iota(jnp.int32, pairs.shape, 1)
     pairs = jnp.where(token % streams == logit % streams, pairs, 0.0)
-    by_token = jnp.dot(
-        group(tokens, streams),
-        jnp.concatenate([pairs, squares], axis=1),
-        preferred_element_type=F32,
-        precision=lax.Precision.HIGHEST,
-    )
+    both = jnp.concatenate([pairs, squares], axis=1)
+    by_token = jnp.sum(both.reshape(tokens, streams, both.shape[1]), axis=1)
     out_ref[:, :logits] = nt(
         by_token[:, : logits * streams], group(logits, streams), lax.Precision.HIGHEST
     )

time: 63.8 us -> 63.6 us (level)
  no operation moved by 1% of the time
where the time goes in v4:
time: 63.6 us; the launch traced here: 63.4 us
  starting transfers between devices  21.8 us (34%)
  Pallas kernels  20.8 us (33%)
  waiting for transfers between devices  19 us (30%)
  other arithmetic  0.9 us (1%)
    ppermute x21, starting transfers between devices, flip(): return lax.ppermute(value, axis, [(i, i ^ bits) for i in range(size)])  21.8 us
    ppermute x21, waiting for transfers between devices, flip(): return lax.ppermute(value, axis, [(i, i ^ bits) for i in range(size)])  19 us
    pallas_call x3, Pallas kernels, load(): call(functools.partial(load_body, spans=spans), tuple((jax.ShapeDtypeStru...  9.17 us
    pallas_call x3, Pallas kernels, layer(): call(functools.partial(expand_body, start=start, spans=spans), outs + ([h...  5.5 us
    pallas_call x1, Pallas kernels, layer(): call(logits_body, (shape((tokens, LANES), F32), shape(streams.shape, BF16...  1.54 us
    pallas_call x2, Pallas kernels, outward(): return call(other_body, outs, [IN_VMEM] * 3, flops=flops)(own, other, down)  1.42 us
    pallas_call x2, Pallas kernels, outward(): call(own_body, shape((part, width), F32), [IN_VMEM] * 2, flops=flops)  1.39 us
  transfers between devices with their start and end apart: 21, of which 9 were waited for; matrix products, arithmetic and copies ran while one was open for 1% of the time, Pallas kernels for 26%

profile of v4, /device:TPU:0, one launch (start us, length us, event | category | flops | bytes accessed | tf_op | source)
XLA Modules:
  0.0 63.4 jit_solution(6553316418977197784)
XLA Ops:
  0.0 1.5 %shard_map.64 = (f32[16,128]{1,0:T(8,128)S(1)}, bf16[16,4,1792]{2,1,0:T(4,128)(2,1)S(1)}, f32[1,24]{1,0:T(1,128)S(1)}) custom-call(bf16[16,4,1792]{2,1,0:T(4,128)(2,1)} %streams_hbm.1, bf16[24,4,1792]{2,1,0:T(4,128)(2,1)} %weight_hbm.1, f32[1,24]{1,0:T(1,128)} %bitcast.7), custom_call_target="tpu_custom_call" | custom-call | tf_op jit(solution)/shard_map/pallas_call | solution.py:278
  1.6 2.5 %collective-permute-start.2 = (f32[16,128]{1,0:T(8,128)S(1)}, f32[16,128]{1,0:T(8,128)S(1)}, u32[]{:S(2)}, u32[]{:S(2)}) collective-permute-start(f32[16,128]{1,0:T(8,128)S(1)} %get-tuple-element.43.refs_0_), channel_id=1, source_target_pairs={{0,3},{1,2},{2,1},{3,0},{4,7},{5,6},{6,5},{7,4},{8,11},{9,10},{10,... | collective-permute-start | bytes 24584 | tf_op jit(solution)/shard_map/ppermute | solution.py:44
  5.4 2.3 %collective-permute-done.1.refs_2_ = f32[16,128]{1,0:T(8,128)S(1)} collective-permute-done((f32[16,128]{1,0:T(8,128)S(1)}, f32[16,128]{1,0:T(8,128)S(1)}, u32[]{:S(2)}, u32[]{:S(2)}) %collective-permute-start.1) | collective-permute-done | bytes 8224 | tf_op jit(solution)/shard_map/ppermute | solution.py:44
  7.9 2.7 %collective-permute-start.3 = (bf16[16,1792]{1,0:T(8,128)(2,1)S(1)}, bf16[16,1792]{1,0:T(8,128)(2,1)S(1)}, u32[]{:S(2)}, u32[]{:S(2)}) collective-permute-start(bf16[16,1792]{1,0:T(8,128)(2,1)S(1)} %get-tuple-element.44.after_ref), channel_id=1, source_target_pairs={{0,16},{4,20},{8,24},{12,28},{16,0},{20,4},{24,8},{28,12},{1,17},{... | collective-permute-start | bytes 172040 | tf_op jit(solution)/shard_map/ppermute | solution.py:44
  10.6 2.6 %shard_map.67.refs_2_ = bf16[2304,1792]{1,0:T(8,128)(2,1)S(1)} custom-call(bf16[16,1792]{1,0:T(8,128)(2,1)S(1)} %get-tuple-element.44.after_ref, bf16[2304,1792]{1,0:T(8,128)(2,1)} %refs_0_.6), custom_call_target="tpu_custom_call" | custom-call | flops 2000000000 | tf_op jit(solution)/shard_map/pallas_call | solution.py:181
  13.3 2.5 %collective-permute-start.6 = (bf16[32,1792]{1,0:T(8,128)(2,1)S(1)}, bf16[32,1792]{1,0:T(8,128)(2,1)S(1)}, u32[]{:S(2)}, u32[]{:S(2)}) collective-permute-start(bf16[32,1792]{1,0:T(8,128)(2,1)S(1)} %get-tuple-element.77.after_ref), channel_id=1, source_target_pairs={{0,12},{4,8},{8,4},{12,0},{16,28},{20,24},{24,20},{28,16},{1,13},{... | collective-permute-start | bytes 344072 | tf_op jit(solution)/shard_map/ppermute | solution.py:44
  16.8 3.1 %shard_map.68 = (bf16[2304,1792]{1,0:T(8,128)(2,1)S(1)}, bf16[2304,1792]{1,0:T(8,128)(2,1)S(1)}) custom-call(bf16[32,1792]{1,0:T(8,128)(2,1)S(1)} %get-tuple-element.77.after_ref, bf16[2304,1792]{1,0:T(8,128)(2,1)} %refs_1_.3, bf16[2304,1792]{1,0:T(8,128)(2,1)} %refs_0_.6, bf16[2304,1792]{1,0:T(8,128)(2,1)S(1)} %shard_map.67.refs_2_), custom_call_target="tpu_custom_call", output_to_operand_aliasing={{1}: (3, {})} | custom-call | flops 2000000000 | tf_op jit(solution)/shard_map/pallas_call | solution.py:181
  19.9 1.3 %collective-permute-done.4 = bf16[32,1792]{1,0:T(8,128)(2,1)S(1)} collective-permute-done((bf16[32,1792]{1,0:T(8,128)(2,1)S(1)}, bf16[32,1792]{1,0:T(8,128)(2,1)S(1)}, u32[]{:S(2)}, u32[]{:S(2)}) %collective-permute-start.4) | collective-permute-done | bytes 114720 | tf_op jit(solution)/shard_map/ppermute | solution.py:44
  21.3 2.6 %shard_map.69 = (bf16[2,128,512]{2,1,0:T(8,128)(2,1)S(1)}, f32[2,128,512]{2,1,0:T(8,128)S(1)}, bf16[2304,1792]{1,0:T(8,128)(2,1)S(1)}, bf16[2304,1792]{1,0:T(8,128)(2,1)S(1)}) custom-call(bf16[128,1792]{1,0:T(8,128)(2,1)S(1)} %constant_dynamic-update-slice_fusion.2.after_ref.x_ref, ...), custom_call_target="tpu_custom_call", output_to_operand_aliasing={{2}: (2, {}), {3}: (3, {})} | custom-call | flops 939524096 | tf_op jit(solution)/shard_map/pallas_call | solution.py:330
  23.9 1.6 %shard_map.70 = (bf16[2,128,384]{2,1,0:T(8,128)(2,1)S(1)}, f32[2,128,384]{2,1,0:T(8,128)S(1)}) custom-call(bf16[2,128,512]{2,1,0:T(8,128)(2,1)S(1)} %get-tuple-element.47.after_ref, bf16[128,1792]{1,0:T(8,128)(2,1)S(1)} %constant_dynamic-update-slice_fusion.2.after_ref.x_ref, bf16[2304,1792]{1,0:T(8,128)(2,1)S(1)} %get-tuple-element.48.gate_ref, ...), custom_call_target="tpu_custom_call" | custom-call | flops 704643072 | tf_op jit(solution)/shard_map/pallas_call | solution.py:330
  26.1 1.3 %shard_map.71 = (bf16[2,128,256]{2,1,0:T(8,128)(2,1)S(1)}, f32[2,128,256]{2,1,0:T(8,128)S(1)}) custom-call(bf16[2,128,384]{2,1,0:T(8,128)(2,1)S(1)} %get-tuple-element.50.after_ref, bf16[128,1792]{1,0:T(8,128)(2,1)S(1)} %constant_dynamic-update-slice_fusion.2.after_ref.x_ref, bf16[2304,1792]{1,0:T(8,128)(2,1)S(1)} %get-tuple-element.48.gate_ref, ...), custom_call_target="tpu_custom_call" | custom-call | flops 469762048 | tf_op jit(solution)/shard_map/pallas_call | solution.py:330
  27.6 0.7 %collective-permute-start.10 = (bf16[2,64,512]{2,1,0:T(8,128)(2,1)S(1)}, bf16[2,64,512]{2,1,0:T(8,128)(2,1)S(1)}, u32[]{:S(2)}, u32[]{:S(2)}) collective-permute-start(bf16[2,64,512]{2,1,0:T(8,128)(2,1)S(1)} %get-tuple-element.61), channel_id=1, source_target_pairs={{0,2},{1,3},{2,0},{3,1},{4,6},{5,7},{6,4},{7,5},{8,10},{9,11},{10,... | collective-permute-start | bytes 393224 | tf_op jit(solution)/shard_map/ppermute | solution.py:44
  28.4 1.4 %collective-permute-start.11 = (bf16[2,64,384]{2,1,0:T(8,128)(2,1)S(1)}, bf16[2,64,384]{2,1,0:T(8,128)(2,1)S(1)}, u32[]{:S(2)}, u32[]{:S(2)}) collective-permute-start(bf16[2,64,384]{2,1,0:T(8,128)(2,1)S(1)} %get-tuple-element.63), channel_id=1, source_target_pairs={{0,2},{1,3},{2,0},{3,1},{4,6},{5,7},{6,4},{7,5},{8,10},{9,11},{10,... | collective-permute-start | bytes 294920 | tf_op jit(solution)/shard_map/ppermute | solution.py:44
  29.9 0.7 %collective-permute-start.12 = (bf16[2,64,256]{2,1,0:T(8,128)(2,1)S(1)}, bf16[2,64,256]{2,1,0:T(8,128)(2,1)S(1)}, u32[]{:S(2)}, u32[]{:S(2)}) collective-permute-start(bf16[2,64,256]{2,1,0:T(8,128)(2,1)S(1)} %get-tuple-element.65), channel_id=1, source_target_pairs={{0,2},{1,3},{2,0},{3,1},{4,6},{5,7},{6,4},{7,5},{8,10},{9,11},{10,... | collective-permute-start | bytes 196616 | tf_op jit(solution)/shard_map/ppermute | solution.py:44
  30.6 1.4 %collective-permute-start.14 = (bf16[2,64,1152]{2,1,0:T(8,128)(2,1)S(1)}, bf16[2,64,1152]{2,1,0:T(8,128)(2,1)S(1)}, u32[]{:S(2)}, u32[]{:S(2)}) collective-permute-start(bf16[2,64,1152]{2,1,0:T(8,128)(2,1)S(1)} %get-tuple-element.59.after_ref), channel_id=1, source_target_pairs={{0,2},{1,3},{2,0},{3,1},{4,6},{5,7},{6,4},{7,5},{8,10},{9,11},{10,... | collective-permute-start | bytes 884744 | tf_op jit(solution)/shard_map/ppermute | solution.py:44
  32.0 5.5 %collective-permute-done.12.refs_5_ = bf16[2,64,256]{2,1,0:T(8,128)(2,1)S(1)} collective-permute-done((bf16[2,64,256]{2,1,0:T(8,128)(2,1)S(1)}, bf16[2,64,256]{2,1,0:T(8,128)(2,1)S(1)}, u32[]{:S(2)}, u32[]{:S(2)}) %collective-permute-start.12) | collective-permute-done | bytes 65568 | tf_op jit(solution)/shard_map/ppermute | solution.py:44
  37.7 3.4 %shard_map.76.down_ref = bf16[2304,1792]{1,0:T(8,128)(2,1)S(1)} custom-call(bf16[2,64,1152]{2,1,0:T(8,128)(2,1)S(1)} %get-tuple-element.59.after_ref, bf16[2304,1792]{1,0:T(8,128)(2,1)} %refs_0_.7), custom_call_target="tpu_custom_call" | custom-call | flops 2000000000 | tf_op jit(solution)/shard_map/pallas_call | solution.py:181
  41.2 0.7 %shard_map.77.own_ref = f32[64,1792]{1,0:T(8,128)S(1)} custom-call(bf16[64,1152]{1,0:T(8,128)(2,1)S(1)} %shard_map.75.mine_ref, bf16[2304,1792]{1,0:T(8,128)(2,1)S(1)} %shard_map.76.down_ref), custom_call_target="tpu_custom_call" | custom-call | flops 264241152 | tf_op jit(solution)/shard_map/pallas_call | solution.py:364
  41.9 0.7 %shard_map.78 = (bf16[32,1792]{1,0:T(8,128)(2,1)S(1)}, bf16[32,1792]{1,0:T(8,128)(2,1)S(1)}) custom-call(f32[64,1792]{1,0:T(8,128)S(1)} %shard_map.77.own_ref, bf16[64,1152]{1,0:T(8,128)(2,1)S(1)} %collective-permute-done.13.other_ref, bf16[2304,1792]{1,0:T(8,128)(2,1)S(1)} %shard_map.76.down_ref), custom_call_target="tpu_custom_call" | custom-call | flops 264241152 | tf_op jit(solution)/shard_map/pallas_call | solution.py:365
  42.6 0.8 %collective-permute-done.14.refs_1_ = bf16[2,64,1152]{2,1,0:T(8,128)(2,1)S(1)} collective-permute-done((bf16[2,64,1152]{2,1,0:T(8,128)(2,1)S(1)}, bf16[2,64,1152]{2,1,0:T(8,128)(2,1)S(1)}, u32[]{:S(2)}, u32[]{:S(2)}) %collective-permute-start.14) | collective-permute-done | bytes 294944 | tf_op jit(solution)/shard_map/ppermute | solution.py:44
  43.6 2.3 %collective-permute-start.17 = (bf16[32,1792]{1,0:T(8,128)(2,1)S(1)}, bf16[32,1792]{1,0:T(8,128)(2,1)S(1)}, u32[]{:S(2)}, u32[]{:S(2)}) collective-permute-start(bf16[32,1792]{1,0:T(8,128)(2,1)S(1)} %get-tuple-element.69), channel_id=1, source_target_pairs={{0,12},{4,8},{8,4},{12,0},{16,28},{20,24},{24,20},{28,16},{1,13},{... | collective-permute-start | bytes 344072 | tf_op jit(solution)/shard_map/ppermute | solution.py:44
  46.3 0.7 %shard_map.80.own_ref = f32[64,1792]{1,0:T(8,128)S(1)} custom-call(bf16[64,1152]{1,0:T(8,128)(2,1)S(1)} %shard_map.79.mine_ref, bf16[2304,1792]{1,0:T(8,128)(2,1)S(1)} %shard_map.76.down_ref), custom_call_target="tpu_custom_call" | custom-call | flops 264241152 | tf_op jit(solution)/shard_map/pallas_call | solution.py:364
  47.0 0.7 %shard_map.81 = (f32[32,1792]{1,0:T(8,128)S(1)}, bf16[16,1792]{1,0:T(8,128)(2,1)S(1)}, bf16[16,1792]{1,0:T(8,128)(2,1)S(1)}) custom-call(f32[64,1792]{1,0:T(8,128)S(1)} %shard_map.80.own_ref, bf16[64,1152]{1,0:T(8,128)(2,1)S(1)} %collective-permute-done.15.other_ref, bf16[2304,1792]{1,0:T(8,128)(2,1)S(1)} %shard_map.76.down_ref), custom_call_target="tpu_custom_call" | custom-call | flops 264241152 | tf_op jit(solution)/shard_map/pallas_call | solution.py:365
  47.7 2.8 %collective-permute-done.17.three_ref = bf16[32,1792]{1,0:T(8,128)(2,1)S(1)} collective-permute-done((bf16[32,1792]{1,0:T(8,128)(2,1)S(1)}, bf16[32,1792]{1,0:T(8,128)(2,1)S(1)}, u32[]{:S(2)}, u32[]{:S(2)}) %collective-permute-start.17) | collective-permute-done | bytes 114720 | tf_op jit(solution)/shard_map/ppermute | solution.py:44
  50.5 1.7 %collective-permute-done.16.two_ref = bf16[32,1792]{1,0:T(8,128)(2,1)S(1)} collective-permute-done((bf16[32,1792]{1,0:T(8,128)(2,1)S(1)}, bf16[32,1792]{1,0:T(8,128)(2,1)S(1)}, u32[]{:S(2)}, u32[]{:S(2)}) %collective-permute-start.16) | collective-permute-done | bytes 114720 | tf_op jit(solution)/shard_map/ppermute | solution.py:44
  52.3 2.2 %collective-permute-start.20 = (bf16[16,1792]{1,0:T(8,128)(2,1)S(1)}, bf16[16,1792]{1,0:T(8,128)(2,1)S(1)}, u32[]{:S(2)}, u32[]{:S(2)}) collective-permute-start(bf16[16,1792]{1,0:T(8,128)(2,1)S(1)} %get-tuple-element.70.after_ref), channel_id=1, source_target_pairs={{0,16},{4,20},{8,24},{12,28},{16,0},{20,4},{24,8},{28,12},{1,17},{... | collective-permute-start | bytes 172040 | tf_op jit(solution)/shard_map/ppermute | solution.py:44
  54.5 0.7 %shard_map.83 = f32[16,128]{1,0:T(8,128)S(1)} custom-call(bf16[16,1792]{1,0:T(8,128)(2,1)S(1)} %get-tuple-element.70.after_ref, f32[16,128]{1,0:T(8,128)S(1)} %get-tuple-element.71.logits_ref), custom_call_target="tpu_custom_call" | custom-call | flops 1000000000 | tf_op jit(solution)/shard_map/pallas_call | solution.py:384
  55.4 1.0 %collective-permute-start.18 = (bf16[16,1792]{1,0:T(8,128)(2,1)S(1)}, bf16[16,1792]{1,0:T(8,128)(2,1)S(1)}, u32[]{:S(2)}, u32[]{:S(2)}) collective-permute-start(bf16[16,1792]{1,0:T(8,128)(2,1)S(1)} %get-tuple-element.75), channel_id=1, source_target_pairs={{0,4},{4,0},{8,12},{12,8},{16,20},{20,16},{24,28},{28,24},{1,5},{5... | collective-permute-start | bytes 172040 | tf_op jit(solution)/shard_map/ppermute | solution.py:44
  56.5 1.3 %collective-permute-start.19 = (bf16[16,1792]{1,0:T(8,128)(2,1)S(1)}, bf16[16,1792]{1,0:T(8,128)(2,1)S(1)}, u32[]{:S(2)}, u32[]{:S(2)}) collective-permute-start(bf16[16,1792]{1,0:T(8,128)(2,1)S(1)} %get-tuple-element.76), channel_id=1, source_target_pairs={{0,20},{4,16},{8,28},{12,24},{16,4},{20,0},{24,12},{28,8},{1,21},{... | collective-permute-start | bytes 172040 | tf_op jit(solution)/shard_map/ppermute | solution.py:44
  58.2 1.4 %collective-permute-done.18 = bf16[16,1792]{1,0:T(8,128)(2,1)S(1)} collective-permute-done((bf16[16,1792]{1,0:T(8,128)(2,1)S(1)}, bf16[16,1792]{1,0:T(8,128)(2,1)S(1)}, u32[]{:S(2)}, u32[]{:S(2)}) %collective-permute-start.18) | collective-permute-done | bytes 57376 | tf_op jit(solution)/shard_map/ppermute | solution.py:44
  59.6 2.9 %collective-permute-done.19 = bf16[16,1792]{1,0:T(8,128)(2,1)S(1)} collective-permute-done((bf16[16,1792]{1,0:T(8,128)(2,1)S(1)}, bf16[16,1792]{1,0:T(8,128)(2,1)S(1)}, u32[]{:S(2)}, u32[]{:S(2)}) %collective-permute-start.19) | collective-permute-done | bytes 57376 | tf_op jit(solution)/shard_map/ppermute | solution.py:44
  62.6 0.9 %add_convert_fusion = bf16[16,4,1792]{2,1,0:T(4,128)(2,1)} fusion(f32[16,4,1792]{2,1,0:T(4,128)S(1)} %fusion, f32[16,1792]{1,0:T(8,128)S(1)} %convert_add_fusion, f32[16,4]{1,0:T(8,128)S(1)} %bitcast.5), kind=kLoop, calls=%fused_computation | loop fusion | flops 344064 | bytes 803072 | tf_op jit(solution)/shard_map/convert_element_type | solution.py:401
  (43 shorter events, 5.2 us)
Async XLA Ops:
  1.6 3.9 %collective-permute-start.2 = (f32[16,128]{1,0:T(8,128)S(1)}, f32[16,128]{1,0:T(8,128)S(1)}, u32[]{:S(2)}, u32[]{:S(2)}) collective-permute-start(f32[16,128]{1,0:T(8,128)S(1)} %get-tuple-element.43.refs_0_), channel_id=1, source_target_pairs={{0,3},{1,2},{2,1},{3,0},{4,7},{5,6},{6,5},{7,4},{8,11},{9,10},{10,... | collective-permute-start | bytes 24584 | tf_op jit(solution)/shard_map/ppermute | solution.py:44
  4.1 3.7 %collective-permute-start.1 = (f32[16,128]{1,0:T(8,128)S(1)}, f32[16,128]{1,0:T(8,128)S(1)}, u32[]{:S(2)}, u32[]{:S(2)}) collective-permute-start(f32[16,128]{1,0:T(8,128)S(1)} %get-tuple-element.43.refs_0_), channel_id=1, source_target_pairs={{0,2},{1,3},{2,0},{3,1},{4,6},{5,7},{6,4},{7,5},{8,10},{9,11},{10,... | collective-permute-start | bytes 24584 | tf_op jit(solution)/shard_map/ppermute | solution.py:44
  4.7 3.0 %collective-permute-start = (f32[16,128]{1,0:T(8,128)S(1)}, f32[16,128]{1,0:T(8,128)S(1)}, u32[]{:S(2)}, u32[]{:S(2)}) collective-permute-start(f32[16,128]{1,0:T(8,128)S(1)} %get-tuple-element.43.refs_0_), channel_id=1, source_target_pairs={{0,1},{1,0},{2,3},{3,2},{4,5},{5,4},{6,7},{7,6},{8,9},{9,8},{10,11... | collective-permute-start | bytes 24584 | tf_op jit(solution)/shard_map/ppermute | solution.py:44
  7.9 5.3 %collective-permute-start.3 = (bf16[16,1792]{1,0:T(8,128)(2,1)S(1)}, bf16[16,1792]{1,0:T(8,128)(2,1)S(1)}, u32[]{:S(2)}, u32[]{:S(2)}) collective-permute-start(bf16[16,1792]{1,0:T(8,128)(2,1)S(1)} %get-tuple-element.44.after_ref), channel_id=1, source_target_pairs={{0,16},{4,20},{8,24},{12,28},{16,0},{20,4},{24,8},{28,12},{1,17},{... | collective-permute-start | bytes 172040 | tf_op jit(solution)/shard_map/ppermute | solution.py:44
  13.3 8.0 %collective-permute-start.6 = (bf16[32,1792]{1,0:T(8,128)(2,1)S(1)}, bf16[32,1792]{1,0:T(8,128)(2,1)S(1)}, u32[]{:S(2)}, u32[]{:S(2)}) collective-permute-start(bf16[32,1792]{1,0:T(8,128)(2,1)S(1)} %get-tuple-element.77.after_ref), channel_id=1, source_target_pairs={{0,12},{4,8},{8,4},{12,0},{16,28},{20,24},{24,20},{28,16},{1,13},{... | collective-permute-start | bytes 344072 | tf_op jit(solution)/shard_map/ppermute | solution.py:44
  15.8 5.4 %collective-permute-start.5 = (bf16[32,1792]{1,0:T(8,128)(2,1)S(1)}, bf16[32,1792]{1,0:T(8,128)(2,1)S(1)}, u32[]{:S(2)}, u32[]{:S(2)}) collective-permute-start(bf16[32,1792]{1,0:T(8,128)(2,1)S(1)} %get-tuple-element.77.after_ref), channel_id=1, source_target_pairs={{0,8},{4,12},{8,0},{12,4},{16,24},{20,28},{24,16},{28,20},{1,9},{5... | collective-permute-start | bytes 344072 | tf_op jit(solution)/shard_map/ppermute | solution.py:44
  16.3 4.9 %collective-permute-start.4 = (bf16[32,1792]{1,0:T(8,128)(2,1)S(1)}, bf16[32,1792]{1,0:T(8,128)(2,1)S(1)}, u32[]{:S(2)}, u32[]{:S(2)}) collective-permute-start(bf16[32,1792]{1,0:T(8,128)(2,1)S(1)} %get-tuple-element.77.after_ref), channel_id=1, source_target_pairs={{0,4},{4,0},{8,12},{12,8},{16,20},{20,16},{24,28},{28,24},{1,5},{5... | collective-permute-start | bytes 344072 | tf_op jit(solution)/shard_map/ppermute | solution.py:44
  23.9 3.7 %collective-permute-start.9 = (bf16[2,128,512]{2,1,0:T(8,128)(2,1)S(1)}, bf16[2,128,512]{2,1,0:T(8,128)(2,1)S(1)}, u32[]{:S(2)}, u32[]{:S(2)}) collective-permute-start(bf16[2,128,512]{2,1,0:T(8,128)(2,1)S(1)} %get-tuple-element.47.after_ref), channel_id=1, source_target_pairs={{0,1},{1,0},{2,3},{3,2},{4,5},{5,4},{6,7},{7,6},{8,9},{9,8},{10,11... | collective-permute-start | bytes 786440 | tf_op jit(solution)/shard_map/ppermute | solution.py:44
  25.6 2.7 %collective-permute-start.8 = (bf16[2,128,384]{2,1,0:T(8,128)(2,1)S(1)}, bf16[2,128,384]{2,1,0:T(8,128)(2,1)S(1)}, u32[]{:S(2)}, u32[]{:S(2)}) collective-permute-start(bf16[2,128,384]{2,1,0:T(8,128)(2,1)S(1)} %get-tuple-element.50.after_ref), channel_id=1, source_target_pairs={{0,1},{1,0},{2,3},{3,2},{4,5},{5,4},{6,7},{7,6},{8,9},{9,8},{10,11... | collective-permute-start | bytes 589832 | tf_op jit(solution)/shard_map/ppermute | solution.py:44
  27.4 2.4 %collective-permute-start.7 = (bf16[2,128,256]{2,1,0:T(8,128)(2,1)S(1)}, bf16[2,128,256]{2,1,0:T(8,128)(2,1)S(1)}, u32[]{:S(2)}, u32[]{:S(2)}) collective-permute-start(bf16[2,128,256]{2,1,0:T(8,128)(2,1)S(1)} %get-tuple-element.52), channel_id=1, source_target_pairs={{0,1},{1,0},{2,3},{3,2},{4,5},{5,4},{6,7},{7,6},{8,9},{9,8},{10,11... | collective-permute-start | bytes 393224 | tf_op jit(solution)/shard_map/ppermute | solution.py:44
  27.6 10.0 %collective-permute-start.10 = (bf16[2,64,512]{2,1,0:T(8,128)(2,1)S(1)}, bf16[2,64,512]{2,1,0:T(8,128)(2,1)S(1)}, u32[]{:S(2)}, u32[]{:S(2)}) collective-permute-start(bf16[2,64,512]{2,1,0:T(8,128)(2,1)S(1)} %get-tuple-element.61), channel_id=1, source_target_pairs={{0,2},{1,3},{2,0},{3,1},{4,6},{5,7},{6,4},{7,5},{8,10},{9,11},{10,... | collective-permute-start | bytes 393224 | tf_op jit(solution)/shard_map/ppermute | solution.py:44
  28.4 9.2 %collective-permute-start.11 = (bf16[2,64,384]{2,1,0:T(8,128)(2,1)S(1)}, bf16[2,64,384]{2,1,0:T(8,128)(2,1)S(1)}, u32[]{:S(2)}, u32[]{:S(2)}) collective-permute-start(bf16[2,64,384]{2,1,0:T(8,128)(2,1)S(1)} %get-tuple-element.63), channel_id=1, source_target_pairs={{0,2},{1,3},{2,0},{3,1},{4,6},{5,7},{6,4},{7,5},{8,10},{9,11},{10,... | collective-permute-start | bytes 294920 | tf_op jit(solution)/shard_map/ppermute | solution.py:44
  29.9 7.6 %collective-permute-start.12 = (bf16[2,64,256]{2,1,0:T(8,128)(2,1)S(1)}, bf16[2,64,256]{2,1,0:T(8,128)(2,1)S(1)}, u32[]{:S(2)}, u32[]{:S(2)}) collective-permute-start(bf16[2,64,256]{2,1,0:T(8,128)(2,1)S(1)} %get-tuple-element.65), channel_id=1, source_target_pairs={{0,2},{1,3},{2,0},{3,1},{4,6},{5,7},{6,4},{7,5},{8,10},{9,11},{10,... | collective-permute-start | bytes 196616 | tf_op jit(solution)/shard_map/ppermute | solution.py:44
  30.6 12.7 %collective-permute-start.14 = (bf16[2,64,1152]{2,1,0:T(8,128)(2,1)S(1)}, bf16[2,64,1152]{2,1,0:T(8,128)(2,1)S(1)}, u32[]{:S(2)}, u32[]{:S(2)}) collective-permute-start(bf16[2,64,1152]{2,1,0:T(8,128)(2,1)S(1)} %get-tuple-element.59.after_ref), channel_id=1, source_target_pairs={{0,2},{1,3},{2,0},{3,1},{4,6},{5,7},{6,4},{7,5},{8,10},{9,11},{10,... | collective-permute-start | bytes 884744 | tf_op jit(solution)/shard_map/ppermute | solution.py:44
  37.6 4.2 %collective-permute-start.13 = (bf16[64,1152]{1,0:T(8,128)(2,1)S(1)}, bf16[64,1152]{1,0:T(8,128)(2,1)S(1)}, u32[]{:S(2)}, u32[]{:S(2)}) collective-permute-start(bf16[64,1152]{1,0:T(8,128)(2,1)S(1)} %shard_map.75.mine_ref), channel_id=1, source_target_pairs={{0,1},{1,0},{2,3},{3,2},{4,5},{5,4},{6,7},{7,6},{8,9},{9,8},{10,11... | collective-permute-start | bytes 442376 | tf_op jit(solution)/shard_map/ppermute | solution.py:44
  43.5 3.5 %collective-permute-start.15 = (bf16[64,1152]{1,0:T(8,128)(2,1)S(1)}, bf16[64,1152]{1,0:T(8,128)(2,1)S(1)}, u32[]{:S(2)}, u32[]{:S(2)}) collective-permute-start(bf16[64,1152]{1,0:T(8,128)(2,1)S(1)} %shard_map.79.mine_ref), channel_id=1, source_target_pairs={{0,1},{1,0},{2,3},{3,2},{4,5},{5,4},{6,7},{7,6},{8,9},{9,8},{10,11... | collective-permute-start | bytes 442376 | tf_op jit(solution)/shard_map/ppermute | solution.py:44
  43.6 7.0 %collective-permute-start.17 = (bf16[32,1792]{1,0:T(8,128)(2,1)S(1)}, bf16[32,1792]{1,0:T(8,128)(2,1)S(1)}, u32[]{:S(2)}, u32[]{:S(2)}) collective-permute-start(bf16[32,1792]{1,0:T(8,128)(2,1)S(1)} %get-tuple-element.69), channel_id=1, source_target_pairs={{0,12},{4,8},{8,4},{12,0},{16,28},{20,24},{24,20},{28,16},{1,13},{... | collective-permute-start | bytes 344072 | tf_op jit(solution)/shard_map/ppermute | solution.py:44
  45.9 6.4 %collective-permute-start.16 = (bf16[32,1792]{1,0:T(8,128)(2,1)S(1)}, bf16[32,1792]{1,0:T(8,128)(2,1)S(1)}, u32[]{:S(2)}, u32[]{:S(2)}) collective-permute-start(bf16[32,1792]{1,0:T(8,128)(2,1)S(1)} %get-tuple-element.66.after_ref), channel_id=1, source_target_pairs={{0,8},{4,12},{8,0},{12,4},{16,24},{20,28},{24,16},{28,20},{1,9},{5... | collective-permute-start | bytes 344072 | tf_op jit(solution)/shard_map/ppermute | solution.py:44
  47.0 10.7 %copy-start = (bf16[16,4,1792]{2,1,0:T(4,128)(2,1)S(1)}, bf16[16,4,1792]{2,1,0:T(4,128)(2,1)}, u32[]{:S(2)}) copy-start(bf16[16,4,1792]{2,1,0:T(4,128)(2,1)} %streams_hbm.1) | copy-start | bytes 688132
  52.3 6.0 %collective-permute-start.20 = (bf16[16,1792]{1,0:T(8,128)(2,1)S(1)}, bf16[16,1792]{1,0:T(8,128)(2,1)S(1)}, u32[]{:S(2)}, u32[]{:S(2)}) collective-permute-start(bf16[16,1792]{1,0:T(8,128)(2,1)S(1)} %get-tuple-element.70.after_ref), channel_id=1, source_target_pairs={{0,16},{4,20},{8,24},{12,28},{16,0},{20,4},{24,8},{28,12},{1,17},{... | collective-permute-start | bytes 172040 | tf_op jit(solution)/shard_map/ppermute | solution.py:44
  55.4 4.2 %collective-permute-start.18 = (bf16[16,1792]{1,0:T(8,128)(2,1)S(1)}, bf16[16,1792]{1,0:T(8,128)(2,1)S(1)}, u32[]{:S(2)}, u32[]{:S(2)}) collective-permute-start(bf16[16,1792]{1,0:T(8,128)(2,1)S(1)} %get-tuple-element.75), channel_id=1, source_target_pairs={{0,4},{4,0},{8,12},{12,8},{16,20},{20,16},{24,28},{28,24},{1,5},{5... | collective-permute-start | bytes 172040 | tf_op jit(solution)/shard_map/ppermute | solution.py:44
  56.5 6.1 %collective-permute-start.19 = (bf16[16,1792]{1,0:T(8,128)(2,1)S(1)}, bf16[16,1792]{1,0:T(8,128)(2,1)S(1)}, u32[]{:S(2)}, u32[]{:S(2)}) collective-permute-start(bf16[16,1792]{1,0:T(8,128)(2,1)S(1)} %get-tuple-element.76), channel_id=1, source_target_pairs={{0,20},{4,16},{8,28},{12,24},{16,4},{20,0},{24,12},{28,8},{1,21},{... | collective-permute-start | bytes 172040 | tf_op jit(solution)/shard_map/ppermute | solution.py:44
